TPU v7x, 32 devices: a whole 2x2x4 slice. The times are simulated.
32 devices in a mesh: span: 8 (over z, x), chord: 4 (over y, core).
Axes of the slice: x: 2, y: 2, z: 4, core: 2. Of those that a mesh axis runs over, the one named last changes fastest.
Arguments:
- fluid_state: float32 [4, 256, 128, 128], P(None, 'span', 'chord'), may hold values from -6 to 6
- shell_disp: float32 [3, 1024, 512], P(None, 'span', 'chord'), may hold values from -6 to 6
- shell_vel: float32 [3, 1024, 512], P(None, 'span', 'chord'), may hold values from -6 to 6
- owners: int32 [32768, 4], P(('span', 'chord')), may hold values from 0 to 31, all different within a row; in each aligned block of 1024 rows (0 to 1023, 1024 to 2047, ...) at most 256 rows name the same one
- node_local: int32 [32768, 4], P(('span', 'chord')), may hold values from 0 to 16383
- rbf_weight: float32 [32768, 4], P(('span', 'chord')), may hold values from 0.2 to 1
- normals: float32 [3, 32768], P(None, ('span', 'chord')), may hold values from -6 to 6
Outputs:
- fluid_next: float32 [4, 256, 128, 128], P(None, 'span', 'chord')
- interface_motion: float32 [6, 32768], P(None, ('span', 'chord'))
- disp_next: float32 [3, 1024, 512], P(None, 'span', 'chord')
- vel_next: float32 [3, 1024, 512], P(None, 'span', 'chord')
Inputs may be any that keep to these rules, and one draw needn't show every extreme that they name: Each interface point names 4 different owners; the points of one device name no owner more than 256 times, a bound that some block reaches.
All inputs are finite; a program needn't handle non-finite values.
Results may differ from a plain program's by a relative error of at most 0.00007.
Values sent between devices are 32-bit elements; how exact they have to be, the bound alone decides.
No kernel may reach another device: no remote copies, remote signals or barrier semaphores. Data moves between devices by JAX's collectives and lax.ppermute only.
A program may use at most 64 MiB of HBM per device.

v0:
```python
import functools

import jax
import jax.numpy as jnp
from jax import lax
from jax.experimental import pallas as pl
from jax.experimental.pallas import tpu as pltpu
from jax.sharding import PartitionSpec as P


flow_speed = 0.5
time_step = 0.4
stiffness = 0.5
damping = 0.2
shell_step = 0.3

AXES = ("span", "chord")
LANES = 128
f32 = jnp.float32
bf16 = jnp.bfloat16
i32 = jnp.int32
NT = (((1,), (1,)), ((), ()))
TN = (((0,), (0,)), ((), ()))
NN = (((1,), (0,)), ((), ()))


def dot(a, b, dims, precision=None):
    return lax.dot_general(a, b, dims, precision=precision, preferred_element_type=f32)


def iota(shape, dim):
    return lax.broadcasted_iota(i32, shape, dim)


def split(value):
    high = value.astype(bf16)
    low = (value - high.astype(f32)).astype(bf16)
    return high, low


def near(value):
    return pltpu.with_memory_space_constraint(value, pltpu.VMEM)


def call(kernel, outs, *args, flops=1_000_000, held=(), **kw):
    single = not isinstance(outs, (list, tuple))
    space = pl.BlockSpec(memory_space=pltpu.VMEM)
    kw.setdefault("in_specs", [space] * len(args))
    args = [near(a) if n in held else a for n, a in enumerate(args)]
    kw.setdefault("out_specs", space if single else [space] * len(outs))
    nbytes = sum(a.size * a.dtype.itemsize for a in args)
    return pl.pallas_call(
        kernel,
        out_shape=outs,
        cost_estimate=pl.CostEstimate(flops=flops, transcendentals=0, bytes_accessed=nbytes),
        **kw,
    )(*args)


def route_kernel(devices, capacity, own_ref, node_ref, req_ref, dest_ref):
    stencil, points = own_ref.shape
    blocks = points // LANES
    rows = req_ref.shape[0]
    member = []
    for b in range(blocks):
        ids = iota((devices, LANES), 0)
        hit = jnp.zeros((devices, LANES), f32)
        for k in range(stencil):
            hit = jnp.where(own_ref[k : k + 1, b * LANES : (b + 1) * LANES] == ids, 1.0, hit)
        member.append(hit)
    stacked = jnp.concatenate(member, axis=0).astype(bf16)
    source = iota((LANES, 2 * LANES), 0)
    target = iota((LANES, 2 * LANES), 1)
    table = jnp.where((source < target) | (target >= LANES), 1.0, 0.0).astype(bf16)
    counted = dot(stacked, table, NN)
    offset = jnp.zeros((devices, LANES), f32)
    for b in range(blocks):
        part = counted[b * devices : (b + 1) * devices]
        rank = part[:, :LANES] + offset
        offset = offset + part[:, LANES:]
        ids = iota((devices, LANES), 0)
        for k in range(stencil):
            own = own_ref[k : k + 1, b * LANES : (b + 1) * LANES]
            mine = jnp.sum(jnp.where(own == ids, rank, 0.0), axis=0, keepdims=True)
            dest_ref[k : k + 1, b * LANES : (b + 1) * LANES] = own * capacity + mine.astype(i32)
    total = jnp.zeros((2 * rows, LANES), f32)
    for k in range(stencil):
        dest = dest_ref[k : k + 1, :]
        node = node_ref[k : k + 1, :]
        place = iota((rows, points), 0) == dest // LANES
        upper = (node // LANES + 1).astype(f32)
        lower = (node % LANES).astype(f32)
        left = jnp.concatenate(
            [jnp.where(place, upper, 0.0), jnp.where(place, lower, 0.0)], axis=0
        ).astype(bf16)
        right = jnp.where(iota((LANES, points), 0) == dest % LANES, 1.0, 0.0).astype(bf16)
        total = total + dot(left, right, NT)
    req_ref[...] = (total[:rows] * LANES + total[rows:]).astype(i32)


def slots_kernel(dest_ref, weight_ref, slots_ref):
    stencil, points = dest_ref.shape
    rows = slots_ref.shape[1]
    total = jnp.zeros((4 * rows, LANES), f32)
    point = iota((1, points), 1)
    point_a = (point // LANES).astype(f32)
    point_b = (point % LANES).astype(f32)
    for k in range(stencil):
        dest = dest_ref[k : k + 1, :]
        high, low = split(weight_ref[k : k + 1, :])
        place = iota((rows, points), 0) == dest // LANES
        parts = [point_a, point_b, high.astype(f32), low.astype(f32)]
        left = jnp.concatenate([jnp.where(place, part, 0.0) for part in parts], axis=0)
        right = jnp.where(iota((LANES, points), 0) == dest % LANES, 1.0, 0.0).astype(bf16)
        total = total + dot(left.astype(bf16), right, NT)
    slots_ref[0] = total[:rows]
    slots_ref[1] = total[rows : 2 * rows]
    slots_ref[2] = total[2 * rows : 3 * rows] + total[3 * rows :]


def table_kernel(disp_ref, vel_ref, table_ref):
    nodes, width = disp_ref.shape[1], disp_ref.shape[2]
    half = width // 2
    for c in range(6):
        field = disp_ref[c] if c < 3 else vel_ref[c - 3]
        for n, part in enumerate(split(field.T)):
            for h in range(2):
                first = (6 * n + c) * half
                table_ref[first : first + half, h * nodes : (h + 1) * nodes] = part[
                    h * half : (h + 1) * half
                ]


def pair(ref, first, start=None):
    if start is None:
        return jnp.concatenate([ref[pl.ds(first, 1), :], ref[pl.ds(first + 1, 1), :]], axis=1)
    return jnp.concatenate(
        [ref[start, pl.ds(first, 1), :], ref[start, pl.ds(first + 1, 1), :]], axis=1
    )


def position(chunk_rows, channels, rows, channel, row):
    if chunk_rows:
        return (row // chunk_rows) * (channels * chunk_rows) + channel * chunk_rows + row % chunk_rows
    return channel * rows + row


def fetch_kernel(chunk_rows, group, asked_ref, table_ref, out_ref):
    rows = asked_ref.shape[0]
    half = table_ref.shape[0] // 12
    double = table_ref.shape[1]
    nodes = double // 2

    def step(g, carry):
        for s in range(group):
            t = g * group + s
            asked = pair(asked_ref, 2 * t)
            lower = asked % LANES
            upper = asked // LANES - 1
            second = lower >= half
            at = jnp.where(upper < 0, -1, jnp.where(second, upper + nodes, upper))
            hot = jnp.where(iota((double, 2 * LANES), 0) == at, 1.0, 0.0).astype(bf16)
            picked = dot(table_ref[...], hot, NN)
            picked = picked[: 6 * half] + picked[6 * half :]
            keep = iota((half, 2 * LANES), 0) == jnp.where(second, lower - half, lower)
            for c in range(6):
                found = jnp.sum(
                    jnp.where(keep, picked[c * half : (c + 1) * half], 0.0), axis=0, keepdims=True
                )
                for h in range(2):
                    to = position(chunk_rows, 6, rows, c, 2 * t + h)
                    out_ref[pl.ds(to, 1), :] = found[:, h * LANES : (h + 1) * LANES]
        return carry

    lax.fori_loop(0, rows // (2 * group), step, 0)


def meet_kernel(
    chunk_rows, group, factor, got_ref, slots_ref, base_ref, normals_ref, motion_ref, wall_ref, out_ref,
    hot_ref,
):
    rows = slots_ref.shape[1]
    blocks = base_ref.shape[0]

    def gather(g, total):
        lefts, hots = [], []
        for s in range(group):
            row = g * group + s
            weight = slots_ref[2, pl.ds(row, 1), :]
            mine = iota((blocks, LANES), 0).astype(f32) == slots_ref[0, pl.ds(row, 1), :]
            hot = jnp.where(
                iota((LANES, LANES), 0).astype(f32) == slots_ref[1, pl.ds(row, 1), :], 1.0, 0.0
            ).astype(bf16)
            left = []
            for c in range(6):
                value = got_ref[pl.ds(position(chunk_rows, 6, rows, c, row), 1), :]
                for part in split(value * weight):
                    left.append(jnp.where(mine, part.astype(f32), 0.0))
            lefts.append(jnp.concatenate(left, axis=0).astype(bf16))
            hots.append(hot)
        hot = jnp.concatenate(hots, axis=1)
        hot_ref[g] = hot
        return total + dot(jnp.concatenate(lefts, axis=1), hot, NT)

    total = lax.fori_loop(0, rows // group, gather, jnp.zeros((12 * blocks, LANES), f32))
    for c in range(6):
        value = total[2 * c * blocks : (2 * c + 1) * blocks] + total[(2 * c + 1) * blocks : (2 * c + 2) * blocks]
        for a in range(blocks):
            motion_ref[c : c + 1, a * LANES : (a + 1) * LANES] = value[a : a + 1]
    wall = value
    wall_ref[...] = wall
    pressure = base_ref[...] + factor * wall
    left = []
    for c in range(3):
        normal = jnp.concatenate(
            [normals_ref[c : c + 1, a * LANES : (a + 1) * LANES] for a in range(blocks)], axis=0
        )
        left.extend(part.astype(f32) for part in split(normal * pressure))
    left = jnp.concatenate(left, axis=0).astype(bf16)

    def spread(g, carry):
        seen = dot(left, hot_ref[g], NN)
        for s in range(group):
            row = g * group + s
            at = slice(s * LANES, (s + 1) * LANES)
            weight = slots_ref[2, pl.ds(row, 1), :]
            mine = iota((blocks, LANES), 0).astype(f32) == slots_ref[0, pl.ds(row, 1), :]
            for c in range(3):
                both = (
                    seen[2 * c * blocks : (2 * c + 1) * blocks, at]
                    + seen[(2 * c + 1) * blocks : (2 * c + 2) * blocks, at]
                )
                load = weight * jnp.sum(jnp.where(mine, both, 0.0), axis=0, keepdims=True)
                out_ref[pl.ds(position(chunk_rows, 3, rows, c, row), 1), :] = load
        return carry

    lax.fori_loop(0, rows // group, spread, 0)


def force_kernel(chunk_rows, group, got_ref, asked_ref, base_ref, disp_ref, disp_out, vel_out, total_ref):
    rows = asked_ref.shape[0]
    nodes, width = disp_ref.shape[1], disp_ref.shape[2]
    half_nodes = nodes // 2
    total_ref[...] = jnp.zeros_like(total_ref)

    def step(g, carry):
        lefts, hots = [], []
        for s in range(group):
            row = g * group + s
            asked = asked_ref[pl.ds(row, 1), :]
            upper = asked // LANES - 1
            lower = asked % LANES
            second = upper >= half_nodes
            place = iota((half_nodes, LANES), 0) == jnp.where(second, upper - half_nodes, upper)
            hots.append(
                jnp.where(
                    iota((2 * width, LANES), 0) == jnp.where(second, lower + width, lower), 1.0, 0.0
                ).astype(bf16)
            )
            left = []
            for c in range(3):
                value = got_ref[pl.ds(position(chunk_rows, 3, rows, c, row), 1), :]
                for part in split(value):
                    left.append(jnp.where(place, part.astype(f32), 0.0))
            lefts.append(jnp.concatenate(left, axis=0).astype(bf16))
        total_ref[...] += dot(jnp.concatenate(lefts, axis=1), jnp.concatenate(hots, axis=1), NT)
        return carry

    lax.fori_loop(0, rows // group, step, 0)
    for c in range(3):
        for h in range(2):
            first = total_ref[2 * c * half_nodes : (2 * c + 1) * half_nodes, h * width : (h + 1) * width]
            second = total_ref[(2 * c + 1) * half_nodes : (2 * c + 2) * half_nodes, h * width : (h + 1) * width]
            at = slice(h * half_nodes, (h + 1) * half_nodes)
            vel_next = base_ref[c, at, :] + shell_step * (first + second)
            vel_out[c, at, :] = vel_next
            disp_out[c, at, :] = disp_ref[c, at, :] + shell_step * vel_next


def pack_kernel(
    disp_ref, fluid_ref, span_last, span_first, chord_last, chord_first, sems
):
    fields, cells_x, cells_y, _ = fluid_ref.shape
    nodes, width = disp_ref.shape[1], disp_ref.shape[2]
    copies = []

    def copy(source, target):
        one = pltpu.make_async_copy(source, target, sems.at[len(copies)])
        one.start()
        copies.append(one)

    for c in range(fields):
        copy(fluid_ref.at[c, pl.ds(cells_x - 3, 3)], span_last.at[pl.ds(3 * c, 3)])
        copy(fluid_ref.at[c, pl.ds(0, 3)], span_first.at[pl.ds(3 * c, 3)])
    for n, c in enumerate((0, 2)):
        copy(fluid_ref.at[c, :, pl.ds(cells_y - 8, 8)], chord_last.at[pl.ds(n * cells_x, cells_x)])
        copy(fluid_ref.at[c, :, pl.ds(0, 8)], chord_first.at[pl.ds(n * cells_x, cells_x)])
    for c in range(3):
        field = disp_ref[c]
        turned = field.T
        span_last[3 * fields, c : c + 1, :] = field[nodes - 1 :, :]
        span_first[3 * fields, c : c + 1, :] = field[:1, :]
        chord_last[2 * cells_x, c : c + 1, :] = turned[width - 1 :, :]
        chord_first[2 * cells_x, c : c + 1, :] = turned[:1, :]
    for one in copies:
        one.wait()


def coef(distance):
    size = jnp.abs(distance)
    value = jnp.where(size == 1, 45.0, jnp.where(size == 2, -9.0, jnp.where(size == 3, 1.0, 0.0)))
    return jnp.where(distance < 0, -value, value)


def flow_kernel(
    disp_ref, vel_ref, fluid_ref, before_x, after_x, before_y, after_y,
    next_ref, pressure_ref, surface_ref, shell_ref, wide, tall, normal, held, sems,
):
    fields, cells_x, cells_y, length = fluid_ref.shape
    nodes, width = disp_ref.shape[1], disp_ref.shape[2]
    copies = []

    def copy(source, target):
        one = pltpu.make_async_copy(source, target, sems.at[len(copies)])
        one.start()
        copies.append(one)

    for c in range(fields):
        copy(fluid_ref.at[c], wide.at[c, pl.ds(3, cells_x)])
    for n, c in enumerate((0, 2)):
        copy(fluid_ref.at[c], tall.at[n, :, pl.ds(8, cells_y)])
    for c in range(fields):
        wide[c, 0:3] = before_x[3 * c : 3 * c + 3]
        wide[c, 3 + cells_x : 6 + cells_x] = after_x[3 * c : 3 * c + 3]
    for n in range(2):
        tall[n, :, 0:8, :] = before_y[n * cells_x : (n + 1) * cells_x]
        tall[n, :, 8 + cells_y : 16 + cells_y, :] = after_y[n * cells_x : (n + 1) * cells_x]
    row = iota((nodes, width), 0)
    lane = iota((nodes, width), 1)
    for c in range(3):
        field = disp_ref[c]

        def column(plane, at):
            only = jnp.where(iota((8, width), 0) == c, plane, 0.0)
            place = jnp.where(iota((8, width), 1) == at, 1.0, 0.0).astype(bf16)
            high, low = split(only)
            return dot(high, place, TN) + dot(low, place, TN)

        left = column(before_y[2 * cells_x], 0)
        right = column(after_y[2 * cells_x], width - 1)
        above = jnp.where(row == 0, before_x[3 * fields, c : c + 1, :], pltpu.roll(field, 1, 0))
        below = jnp.where(
            row == nodes - 1, after_x[3 * fields, c : c + 1, :], pltpu.roll(field, nodes - 1, 0)
        )
        west = jnp.where(lane == 0, left, pltpu.roll(field, 1, 1))
        east = jnp.where(lane == width - 1, right, pltpu.roll(field, width - 1, 1))
        bending = above + below + west + east - 4.0 * field
        vel = vel_ref[c]
        shell_ref[c] = vel + shell_step * (stiffness * bending - damping * vel)
    source = iota((length, length), 0)
    target = iota((length, length), 1)
    inner = coef(source - target)
    ghost = jnp.where(source < 3, coef(-(source + 1 + target)), 0.0)
    for one in copies:
        one.wait()
    flat = cells_x * cells_y
    for n, field, table in ((0, 0, inner + ghost), (1, 3, inner - ghost)):
        table = table.astype(bf16)
        high, low = split(wide[field, 3 : 3 + cells_x].reshape(flat, length))
        total = dot(jnp.concatenate([high, low], axis=1), jnp.concatenate([table, table], axis=0), NN)
        normal[n] = (total * (1.0 / 60.0)).reshape(cells_x, cells_y, length)

    def central(window):
        return (
            0.75 * (window(1) - window(-1)) - 0.15 * (window(2) - window(-2))
        ) + (1.0 / 60.0) * (window(3) - window(-3))

    def plane(x):
        def along_x(field):
            return central(lambda offset: wide[field, x + 3 + offset])

        def along_y(slot):
            return central(lambda offset: tall[slot, x, 8 + offset : 8 + offset + cells_y, :])

        x_p = along_x(0)
        x_u = along_x(1)
        pressure_ref[x] = wide[0, x + 3] + time_step * (
            -flow_speed * x_p - (x_u + along_y(1) + normal[1, x])
        )
        held[0, x] = wide[1, x + 3] + time_step * (-flow_speed * x_u - x_p)
        held[1, x] = wide[2, x + 3] + time_step * (-flow_speed * along_x(2) - along_y(0))
        held[2, x] = wide[3, x + 3] + time_step * (-flow_speed * along_x(3) - normal[0, x])

    parts = 4
    size = cells_x // parts
    copies = []
    for part in range(parts):

        def planes(i, carry):
            plane(part * size + 2 * i)
            plane(part * size + 2 * i + 1)
            return carry

        lax.fori_loop(0, size // 2, planes, 0)
        at = pl.ds(part * size, size)
        one = pltpu.make_async_copy(held.at[:, at], next_ref.at[pl.ds(1, 3), at], sems.at[part])
        one.start()
        copies.append(one)
    lead = jnp.where((iota((8, length), 0) == 0) & (iota((8, length), 1) == 0), 1.0, 0.0).astype(bf16)
    blocks = surface_ref.shape[0]
    per = LANES // cells_y
    for b in range(blocks):
        high, low = split(pressure_ref[b * per : (b + 1) * per].reshape(LANES, length))
        found = dot(lead, high, NT) + dot(lead, low, NT)
        surface_ref[b : b + 1, :] = found[:1]
    for one in copies:
        one.wait()


def wall_kernel(wall_ref, pressure_ref, next_in, next_out):
    del next_in
    _, cells_x, cells_y, length = next_out.shape
    target = iota((8, length), 1)
    row = jnp.zeros((8, length), f32)
    for j in range(3):
        row = row + coef(-(j + 1 + target))
    row = jnp.where(iota((8, length), 0) == 0, row, 0.0).astype(bf16)
    per = LANES // cells_y
    for b in range(cells_x // per):
        wall = jnp.where(
            iota((8, LANES), 0) == 0, wall_ref[b : b + 1, :] * (-2.0 * time_step / 60.0), 0.0
        )
        high, low = split(wall)
        added = dot(high, row, TN) + dot(low, row, TN)
        at = slice(b * per, (b + 1) * per)
        next_out[0, at] = pressure_ref[at] + added.reshape(per, cells_y, length)


def exchange(value, devices, channels, chunk_rows, rows, capacity):
    if chunk_rows:
        shape = (devices, 1, channels * chunk_rows * LANES)
        got = lax.all_to_all(value.reshape(shape), AXES, split_axis=0, concat_axis=0, tiled=True)
        return got.reshape(channels * rows, LANES)
    value = value.reshape(channels, devices, capacity).transpose(1, 0, 2)
    got = lax.all_to_all(value, AXES, split_axis=0, concat_axis=0, tiled=True)
    return got.transpose(1, 0, 2).reshape(channels * rows, LANES)


def body(fluid_state, shell_disp, shell_vel, owners, node_local, rbf_weight, normals):
    span_count = lax.axis_size("span")
    chord_count = lax.axis_size("chord")
    devices = span_count * chord_count
    points, stencil = owners.shape
    capacity = max(2, (2 * points * stencil + devices - 1) // devices)
    rows = devices * capacity // LANES
    chunk_rows = capacity // LANES if capacity % LANES == 0 else 0
    blocks = points // LANES
    fields, cells_x, cells_y, length = fluid_state.shape
    _, nodes, width = shell_disp.shape
    sds = jax.ShapeDtypeStruct
    vmem = pl.BlockSpec(memory_space=pltpu.VMEM)
    hbm = pl.BlockSpec(memory_space=pl.ANY)

    near_out = pltpu.VMEM
    requests, dest = call(
        functools.partial(route_kernel, devices, capacity),
        [near_out((rows, LANES), i32), near_out((stencil, points), i32)],
        owners.T,
        node_local.T,
    )
    asked = exchange(requests, devices, 1, chunk_rows, rows, capacity)

    slots = call(
        slots_kernel,
        near_out((3, rows, LANES), f32),
        dest,
        rbf_weight.T,
        held=(0,),
        flops=200_000_000,
    )
    table = call(table_kernel, near_out((6 * width, 2 * nodes), bf16), shell_disp, shell_vel)

    span_shape = near_out((3 * fields + 1, cells_y, length), f32)
    chord_shape = near_out((2 * cells_x + 1, 8, length), f32)
    span_last, span_first, chord_last, chord_first = call(
        pack_kernel,
        [span_shape, span_shape, chord_shape, chord_shape],
        shell_disp,
        fluid_state,
        in_specs=[vmem, hbm],
        scratch_shapes=[pltpu.SemaphoreType.DMA((2 * fields + 4,))],
    )

    def shifted(last, leading, axis, size):
        up = [(i, i + 1) for i in range(size - 1)]
        down = [(i + 1, i) for i in range(size - 1)]
        return lax.ppermute(last, axis, up), lax.ppermute(leading, axis, down)

    before_x, after_x = shifted(span_last, span_first, "span", span_count)
    before_y, after_y = shifted(chord_last, chord_first, "chord", chord_count)

    flow_next, pressure, surface, shell_base = call(
        flow_kernel,
        [
            sds(fluid_state.shape, f32),
            near_out((cells_x, cells_y, length), f32),
            near_out((blocks, LANES), f32),
            near_out(shell_disp.shape, f32),
        ],
        shell_disp,
        shell_vel,
        fluid_state,
        before_x,
        after_x,
        before_y,
        after_y,
        flops=300_000_000,
        held=(0, 1, 3, 4, 5, 6),
        in_specs=[vmem, vmem, hbm, vmem, vmem, vmem, vmem],
        out_specs=[hbm, vmem, vmem, vmem],
        scratch_shapes=[
            pltpu.VMEM((fields, cells_x + 6, cells_y, length), f32),
            pltpu.VMEM((2, cells_x, cells_y + 16, length), f32),
            pltpu.VMEM((2, cells_x, cells_y, length), f32),
            pltpu.VMEM((3, cells_x, cells_y, length), f32),
            pltpu.SemaphoreType.DMA((fields + 2,)),
        ],
    )

    picked = call(
        functools.partial(fetch_kernel, chunk_rows, 4),
        near_out((6 * rows, LANES), f32),
        asked,
        table,
        held=(0, 1),
        flops=3_000_000_000,
    )
    replies = exchange(picked, devices, 6, chunk_rows, rows, capacity)

    wall_first = 2.0 * (-45.0 + 9.0 - 1.0) / 60.0
    interface_motion, wall, loads = call(
        functools.partial(meet_kernel, chunk_rows, 8, -time_step * wall_first),
        [
            sds((6, points), f32),
            near_out((blocks, LANES), f32),
            near_out((3 * rows, LANES), f32),
        ],
        replies,
        slots,
        surface,
        normals,
        held=(0, 1, 2, 3),
        flops=300_000_000,
        scratch_shapes=[pltpu.VMEM((rows // 8, LANES, 8 * LANES), bf16)],
    )
    arrived = exchange(loads, devices, 3, chunk_rows, rows, capacity)

    block = pl.BlockSpec((1, cells_x, cells_y, length), lambda i: (0, 0, 0, 0))
    fluid_next = call(
        wall_kernel,
        sds(fluid_state.shape, f32),
        wall,
        pressure,
        flow_next,
        flops=100_000_000,
        held=(0, 1),
        grid=(1,),
        in_specs=[vmem, vmem, hbm],
        out_specs=block,
        input_output_aliases={2: 0},
    )

    disp_next, vel_next = call(
        functools.partial(force_kernel, chunk_rows, 8),
        [sds(shell_disp.shape, f32), sds(shell_vel.shape, f32)],
        arrived,
        asked,
        shell_base,
        shell_disp,
        held=(0, 1, 2, 3),
        flops=3_000_000_000,
        scratch_shapes=[pltpu.VMEM((3 * nodes, 2 * width), f32)],
    )
    return (fluid_next, interface_motion, disp_next, vel_next)


def solution(mesh):
    placed = (
        P(None, "span", "chord", None),
        P(None, "span", "chord"),
        P(None, "span", "chord"),
        P(AXES, None),
        P(AXES, None),
        P(AXES, None),
        P(None, AXES),
    )

    return jax.shard_map(
        body,
        mesh=mesh,
        in_specs=placed,
        out_specs=(
            P(None, "span", "chord", None),
            P(None, AXES),
            P(None, "span", "chord"),
            P(None, "span", "chord"),
        ),
        check_vma=False,
    )
```

profile of v0, /device:TPU:1, one launch (start us, length us, event | category | flops | bytes accessed | tf_op | source)
XLA Modules:
  0.0 72.4 jit_solution(13000304429396121269)
XLA Ops:
  0.6 2.1 %shard_map.102 = (s32[64,128]{1,0:T(8,128)}, s32[4,1024]{1,0:T(4,128)S(1)}) custom-call(s32[4,1024]{1,0:T(4,128)} %bitcast.13, s32[4,1024]{1,0:T(4,128)} %bitcast.14), custom_call_target="tpu_custom_call" | custom-call | flops 1000000 | bytes 32768 | tf_op jit(solution)/shard_map/pallas_call | solution.py:52
  2.7 7.1 %all-to-all-start = ((s32[32,1,256]{2,1,0:T(1,128)}), s32[32,1,256]{2,1,0:T(1,128)S(1)}, u32[]{:S(2)}, u32[]{:S(2)}) async-start(s32[32,1,256]{2,1,0:T(1,128)} %bitcast.2), calls=%async_computation | async-start | bytes 65536 | tf_op jit(solution)/shard_map/all_to_all | solution.py:442
  9.8 1.2 %shard_map.103.table_ref = bf16[768,256]{1,0:T(8,128)(2,1)S(1)} custom-call(f32[3,128,128]{2,1,0:T(8,128)} %disp_ref.7, f32[3,128,128]{2,1,0:T(8,128)} %vel_ref.3), custom_call_target="tpu_custom_call" | custom-call | flops 1000000 | bytes 393216 | tf_op jit(solution)/shard_map/pallas_call | solution.py:52
  11.0 5.9 %all-to-all-done = s32[32,1,256]{2,1,0:T(1,128)S(1)} async-done(((s32[32,1,256]{2,1,0:T(1,128)}), s32[32,1,256]{2,1,0:T(1,128)S(1)}, u32[]{:S(2)}, u32[]{:S(2)}) %all-to-all-start) | async-done | bytes 32800 | tf_op jit(solution)/shard_map/all_to_all | solution.py:442
  17.0 5.7 %shard_map.104 = f32[384,128]{1,0:T(8,128)} custom-call(s32[64,128]{1,0:T(8,128)S(1)} %bitcast.11, bf16[768,256]{1,0:T(8,128)(2,1)S(1)} %shard_map.103.table_ref), custom_call_target="tpu_custom_call" | custom-call | flops 3000000000 | bytes 425984 | tf_op jit(solution)/shard_map/pallas_call | solution.py:52
  22.7 0.0 copy-start
  22.7 0.0 copy-start.1
  22.7 2.7 %all-to-all-start.1 = ((f32[32,1,1536]{2,1,0:T(1,128)}), f32[32,1,1536]{2,1,0:T(1,128)S(1)}, u32[]{:S(2)}, u32[]{:S(2)}) async-start(f32[32,1,1536]{2,1,0:T(1,128)} %bitcast.4), calls=%async_computation.1 | async-start | bytes 393216 | tf_op jit(solution)/shard_map/all_to_all | solution.py:442
  25.4 2.3 %shard_map.106 = (f32[13,32,128]{2,1,0:T(8,128)S(1)}, f32[13,32,128]{2,1,0:T(8,128)S(1)}, f32[65,8,128]{2,1,0:T(8,128)S(1)}, f32[65,8,128]{2,1,0:T(8,128)S(1)}) custom-call(f32[3,128,128]{2,1,0:T(8,128)} %disp_ref.7, f32[4,32,32,128]{3,2,1,0:T(8,128)} %fluid_ref.3), custom_call_target="tpu_custom_call" | custom-call | flops 1000000 | bytes 2293760 | tf_op jit(solution)/shard_map/pallas_call | solution.py:52
  27.7 3.6 %collective-permute-start.2 = (f32[65,8,128]{2,1,0:T(8,128)S(1)}, f32[65,8,128]{2,1,0:T(8,128)S(1)}, u32[]{:S(2)}, u32[]{:S(2)}) collective-permute-start(f32[65,8,128]{2,1,0:T(8,128)S(1)} %get-tuple-element.23), channel_id=1, source_target_pairs={{0,1},{1,2},{2,3},{4,5},{5,6},{6,7},{8,9},{9,10},{10,11},{12,13},{... | collective-permute-start | bytes 798728 | tf_op jit(solution)/shard_map/ppermute | solution.py:497
  31.3 1.9 %collective-permute-start.3 = (f32[65,8,128]{2,1,0:T(8,128)S(1)}, f32[65,8,128]{2,1,0:T(8,128)S(1)}, u32[]{:S(2)}, u32[]{:S(2)}) collective-permute-start(f32[65,8,128]{2,1,0:T(8,128)S(1)} %get-tuple-element.24), channel_id=1, source_target_pairs={{1,0},{2,1},{3,2},{5,4},{6,5},{7,6},{9,8},{10,9},{11,10},{13,12},{... | collective-permute-start | bytes 798728 | tf_op jit(solution)/shard_map/ppermute | solution.py:497
  33.2 3.1 %collective-permute-start = (f32[13,32,128]{2,1,0:T(8,128)S(1)}, f32[13,32,128]{2,1,0:T(8,128)S(1)}, u32[]{:S(2)}, u32[]{:S(2)}) collective-permute-start(f32[13,32,128]{2,1,0:T(8,128)S(1)} %get-tuple-element.21), channel_id=1, source_target_pairs={{0,4},{4,8},{8,12},{12,16},{16,20},{20,24},{24,28},{1,5},{5,9},{9,... | collective-permute-start | bytes 638984 | tf_op jit(solution)/shard_map/ppermute | solution.py:497
  36.3 1.3 %collective-permute-start.1 = (f32[13,32,128]{2,1,0:T(8,128)S(1)}, f32[13,32,128]{2,1,0:T(8,128)S(1)}, u32[]{:S(2)}, u32[]{:S(2)}) collective-permute-start(f32[13,32,128]{2,1,0:T(8,128)S(1)} %get-tuple-element.22), channel_id=1, source_target_pairs={{4,0},{8,4},{12,8},{16,12},{20,16},{24,20},{28,24},{5,1},{9,5},{13... | collective-permute-start | bytes 638984 | tf_op jit(solution)/shard_map/ppermute | solution.py:497
  37.6 0.0 copy-start.2
  37.7 1.4 %shard_map.105.slots_ref = f32[3,64,128]{2,1,0:T(8,128)S(1)} custom-call(s32[4,1024]{1,0:T(4,128)S(1)} %get-tuple-element.20.dest_ref, f32[4,1024]{1,0:T(4,128)} %bitcast.15), custom_call_target="tpu_custom_call" | custom-call | flops 200000000 | bytes 32768 | tf_op jit(solution)/shard_map/pallas_call | solution.py:52
  39.1 1.2 %collective-permute-done.before_x = f32[13,32,128]{2,1,0:T(8,128)S(1)} collective-permute-done((f32[13,32,128]{2,1,0:T(8,128)S(1)}, f32[13,32,128]{2,1,0:T(8,128)S(1)}, u32[]{:S(2)}, u32[]{:S(2)}) %collective-permute-start) | collective-permute-done | bytes 213024 | tf_op jit(solution)/shard_map/ppermute | solution.py:497
  40.3 4.1 %collective-permute-done.1.after_x = f32[13,32,128]{2,1,0:T(8,128)S(1)} collective-permute-done((f32[13,32,128]{2,1,0:T(8,128)S(1)}, f32[13,32,128]{2,1,0:T(8,128)S(1)}, u32[]{:S(2)}, u32[]{:S(2)}) %collective-permute-start.1) | collective-permute-done | bytes 213024 | tf_op jit(solution)/shard_map/ppermute | solution.py:497
  44.4 0.0 collective-permute-done.2.before_y
  44.4 0.0 collective-permute-done.3.after_y
  44.4 0.0 copy-done
  44.4 0.0 copy-done.1
  44.4 4.6 %shard_map.107 = (f32[4,32,32,128]{3,2,1,0:T(8,128)}, f32[32,32,128]{2,1,0:T(8,128)S(1)}, f32[8,128]{1,0:T(8,128)S(1)}, f32[3,128,128]{2,1,0:T(8,128)S(1)}) custom-call(f32[3,128,128]{2,1,0:T(8,128)S(1)} %copy-done, f32[3,128,128]{2,1,0:T(8,128)S(1)} %copy-done.1, f32[4,32,32,128]{3,2,1,0:T(8,128)} %fluid_ref.3, ...), custom_call_target="tpu_custom_call" | custom-call | flops 300000000 | bytes 3448832 | tf_op jit(solution)/shard_map/pallas_call | solution.py:52
  49.0 0.0 all-to-all-done.1
  49.0 0.0 copy-done.2
  49.0 4.0 %shard_map.108 = (f32[6,1024]{1,0:T(8,128)}, f32[8,128]{1,0:T(8,128)S(1)}, f32[192,128]{1,0:T(8,128)}) custom-call(f32[384,128]{1,0:T(8,128)S(1)} %bitcast.9, f32[3,64,128]{2,1,0:T(8,128)S(1)} %shard_map.105.slots_ref, f32[8,128]{1,0:T(8,128)S(1)} %get-tuple-element.25.base_ref, f32[3,1024]{1,0:T(4,128)S(1)} %copy-done.2), custom_call_target="tpu_custom_call" | custom-call | flops 300000000 | bytes 311296 | tf_op jit(solution)/shard_map/pallas_call | solution.py:52
  53.0 7.4 %all-to-all-start.2 = ((f32[32,1,768]{2,1,0:T(1,128)}), f32[32,1,768]{2,1,0:T(1,128)S(1)}, u32[]{:S(2)}, u32[]{:S(2)}) async-start(f32[32,1,768]{2,1,0:T(1,128)} %bitcast.7), calls=%async_computation.2 | async-start | bytes 196608 | tf_op jit(solution)/shard_map/all_to_all | solution.py:442
  60.4 1.1 %shard_map.109 = f32[4,32,32,128]{3,2,1,0:T(8,128)} custom-call(f32[8,128]{1,0:T(8,128)S(1)} %get-tuple-element.26.wall_ref, f32[32,32,128]{2,1,0:T(8,128)S(1)} %get-tuple-element.27.pressure_ref, f32[4,32,32,128]{3,2,1,0:T(8,128)} %get-tuple-element.28.next_in), custom_call_target="tpu_custom_call", output_to_operand_aliasing={{}: (2, {})} | custom-call | flops 100000000 | bytes 2625536 | tf_op jit(solution)/shard_map/pallas_call | solution.py:52
  61.6 6.5 %all-to-all-done.2 = f32[32,1,768]{2,1,0:T(1,128)S(1)} async-done(((f32[32,1,768]{2,1,0:T(1,128)}), f32[32,1,768]{2,1,0:T(1,128)S(1)}, u32[]{:S(2)}, u32[]{:S(2)}) %all-to-all-start.2) | async-done | bytes 98336 | tf_op jit(solution)/shard_map/all_to_all | solution.py:442
  68.1 4.3 %shard_map.110 = (f32[3,128,128]{2,1,0:T(8,128)}, f32[3,128,128]{2,1,0:T(8,128)}) custom-call(f32[192,128]{1,0:T(8,128)S(1)} %bitcast.10, s32[64,128]{1,0:T(8,128)S(1)} %bitcast.12, f32[3,128,128]{2,1,0:T(8,128)S(1)} %get-tuple-element.31.base_ref, f32[3,128,128]{2,1,0:T(8,128)S(1)} %copy-done), custom_call_target="tpu_custom_call" | custom-call | flops 3000000000 | bytes 524288 | tf_op jit(solution)/shard_map/pallas_call | solution.py:52
Async XLA Ops:
  2.7 14.2 %all-to-all-start = ((s32[32,1,256]{2,1,0:T(1,128)}), s32[32,1,256]{2,1,0:T(1,128)S(1)}, u32[]{:S(2)}, u32[]{:S(2)}) async-start(s32[32,1,256]{2,1,0:T(1,128)} %bitcast.2), calls=%async_computation | async-start | bytes 65536 | tf_op jit(solution)/shard_map/all_to_all | solution.py:442
  22.7 21.7 %copy-start = (f32[3,128,128]{2,1,0:T(8,128)S(1)}, f32[3,128,128]{2,1,0:T(8,128)}, u32[]{:S(2)}) copy-start(f32[3,128,128]{2,1,0:T(8,128)} %disp_ref.7) | copy-start | bytes 589828
  22.7 21.7 %copy-start.1 = (f32[3,128,128]{2,1,0:T(8,128)S(1)}, f32[3,128,128]{2,1,0:T(8,128)}, u32[]{:S(2)}) copy-start(f32[3,128,128]{2,1,0:T(8,128)} %vel_ref.3) | copy-start | bytes 589828
  22.7 26.3 %all-to-all-start.1 = ((f32[32,1,1536]{2,1,0:T(1,128)}), f32[32,1,1536]{2,1,0:T(1,128)S(1)}, u32[]{:S(2)}, u32[]{:S(2)}) async-start(f32[32,1,1536]{2,1,0:T(1,128)} %bitcast.4), calls=%async_computation.1 | async-start | bytes 393216 | tf_op jit(solution)/shard_map/all_to_all | solution.py:442
  27.7 16.6 %collective-permute-start.2 = (f32[65,8,128]{2,1,0:T(8,128)S(1)}, f32[65,8,128]{2,1,0:T(8,128)S(1)}, u32[]{:S(2)}, u32[]{:S(2)}) collective-permute-start(f32[65,8,128]{2,1,0:T(8,128)S(1)} %get-tuple-element.23), channel_id=1, source_target_pairs={{0,1},{1,2},{2,3},{4,5},{5,6},{6,7},{8,9},{9,10},{10,11},{12,13},{... | collective-permute-start | bytes 798728 | tf_op jit(solution)/shard_map/ppermute | solution.py:497
  31.3 13.1 %collective-permute-start.3 = (f32[65,8,128]{2,1,0:T(8,128)S(1)}, f32[65,8,128]{2,1,0:T(8,128)S(1)}, u32[]{:S(2)}, u32[]{:S(2)}) collective-permute-start(f32[65,8,128]{2,1,0:T(8,128)S(1)} %get-tuple-element.24), channel_id=1, source_target_pairs={{1,0},{2,1},{3,2},{5,4},{6,5},{7,6},{9,8},{10,9},{11,10},{13,12},{... | collective-permute-start | bytes 798728 | tf_op jit(solution)/shard_map/ppermute | solution.py:497
  33.2 7.0 %collective-permute-start = (f32[13,32,128]{2,1,0:T(8,128)S(1)}, f32[13,32,128]{2,1,0:T(8,128)S(1)}, u32[]{:S(2)}, u32[]{:S(2)}) collective-permute-start(f32[13,32,128]{2,1,0:T(8,128)S(1)} %get-tuple-element.21), channel_id=1, source_target_pairs={{0,4},{4,8},{8,12},{12,16},{16,20},{20,24},{24,28},{1,5},{5,9},{9,... | collective-permute-start | bytes 638984 | tf_op jit(solution)/shard_map/ppermute | solution.py:497
  36.3 8.0 %collective-permute-start.1 = (f32[13,32,128]{2,1,0:T(8,128)S(1)}, f32[13,32,128]{2,1,0:T(8,128)S(1)}, u32[]{:S(2)}, u32[]{:S(2)}) collective-permute-start(f32[13,32,128]{2,1,0:T(8,128)S(1)} %get-tuple-element.22), channel_id=1, source_target_pairs={{4,0},{8,4},{12,8},{16,12},{20,16},{24,20},{28,24},{5,1},{9,5},{13... | collective-permute-start | bytes 638984 | tf_op jit(solution)/shard_map/ppermute | solution.py:497
  37.6 11.3 %copy-start.2 = (f32[3,1024]{1,0:T(4,128)S(1)}, f32[3,1024]{1,0:T(4,128)}, u32[]{:S(2)}) copy-start(f32[3,1024]{1,0:T(4,128)} %normals_ref.1) | copy-start | bytes 36868
  53.0 15.1 %all-to-all-start.2 = ((f32[32,1,768]{2,1,0:T(1,128)}), f32[32,1,768]{2,1,0:T(1,128)S(1)}, u32[]{:S(2)}, u32[]{:S(2)}) async-start(f32[32,1,768]{2,1,0:T(1,128)} %bitcast.7), calls=%async_computation.2 | async-start | bytes 196608 | tf_op jit(solution)/shard_map/all_to_all | solution.py:442
where the time goes:
time: 73.4 us; the launch traced here: 72.4 us
  starting transfers between devices  27.1 us (37%)
  Pallas kernels  26.8 us (37%)
  waiting for transfers between devices  17.7 us (24%)
  between operations  0.76 us (1%)
    pallas_call x9, Pallas kernels, call(): pl.pallas_call(kernel, out_shape=outs, cost_estimate=pl.CostEstimate(flop...  26.8 us
    all_to_all x3, starting transfers between devices, exchange(): lax.all_to_all(value.reshape(shape), AXES, split_axis=0, concat_axis=0, t...  17.2 us
    all_to_all x3, waiting for transfers between devices, exchange(): lax.all_to_all(value.reshape(shape), AXES, split_axis=0, concat_axis=0, t...  12.4 us
    ppermute x4, starting transfers between devices, shifted(): return (lax.ppermute(last, axis, up), lax.ppermute(leading, axis, down))  9.89 us
    ppermute x4, waiting for transfers between devices, shifted(): return (lax.ppermute(last, axis, up), lax.ppermute(leading, axis, down))  5.27 us
  transfers between devices with their start and end apart: 7, of which 4 were waited for; matrix products, arithmetic and copies ran while one was open for 0% of the time, Pallas kernels for 15%

commit v1 on v0

--- a/solution.py
+++ b/solution.py
@@ -57,7 +57,31 @@
     )(*args)
 
 
-def route_kernel(devices, capacity, own_ref, node_ref, req_ref, dest_ref):
+def route_kernel(
+    devices, capacity, own_ref, node_ref, disp_hbm, vel_hbm, fluid_ref,
+    req_hbm, dest_ref, table_ref, span_a, span_b, chord_a, chord_b,
+    req_ref, disp_ref, vel_ref, sems,
+):
+    fields, cells_x, cells_y, _ = fluid_ref.shape
+    copies = []
+
+    def copy(source, target):
+        one = pltpu.make_async_copy(source, target, sems.at[len(copies)])
+        one.start()
+        copies.append(one)
+
+    copy(disp_hbm, disp_ref)
+    copy(vel_hbm, vel_ref)
+    odd_x = lax.axis_index("span") % 2
+    odd_y = lax.axis_index("chord") % 2
+    for c in range(fields):
+        copy(fluid_ref.at[c, pl.ds((1 - odd_x) * (cells_x - 3), 3)], span_a.at[pl.ds(3 * c, 3)])
+        copy(fluid_ref.at[c, pl.ds(odd_x * (cells_x - 3), 3)], span_b.at[pl.ds(3 * c, 3)])
+    for n, c in enumerate((0, 2)):
+        first = pl.multiple_of((1 - odd_y) * (cells_y - 8), 8)
+        copy(fluid_ref.at[c, :, pl.ds(first, 8)], chord_a.at[pl.ds(n * cells_x, cells_x)])
+        first = pl.multiple_of(odd_y * (cells_y - 8), 8)
+        copy(fluid_ref.at[c, :, pl.ds(first, 8)], chord_b.at[pl.ds(n * cells_x, cells_x)])
     stencil, points = own_ref.shape
     blocks = points // LANES
     rows = req_ref.shape[0]
@@ -96,6 +120,29 @@
         right = jnp.where(iota((LANES, points), 0) == dest % LANES, 1.0, 0.0).astype(bf16)
         total = total + dot(left, right, NT)
     req_ref[...] = (total[:rows] * LANES + total[rows:]).astype(i32)
+    copy(req_ref, req_hbm)
+    copies[0].wait()
+    copies[1].wait()
+    nodes, width = disp_ref.shape[1], disp_ref.shape[2]
+    half = width // 2
+    for c in range(6):
+        field = disp_ref[c] if c < 3 else vel_ref[c - 3]
+        turned = field.T
+        if c < 3:
+            ends = (field[nodes - 1 :, :], field[:1, :])
+            span_a[3 * fields, c : c + 1, :] = jnp.where(odd_x == 0, *ends)
+            span_b[3 * fields, c : c + 1, :] = jnp.where(odd_x == 1, *ends)
+            ends = (turned[width - 1 :, :], turned[:1, :])
+            chord_a[2 * cells_x, c : c + 1, :] = jnp.where(odd_y == 0, *ends)
+            chord_b[2 * cells_x, c : c + 1, :] = jnp.where(odd_y == 1, *ends)
+        for n, part in enumerate(split(turned)):
+            for h in range(2):
+                first = (6 * n + c) * half
+                table_ref[first : first + half, h * nodes : (h + 1) * nodes] = part[
+                    h * half : (h + 1) * half
+                ]
+    for one in copies[2:]:
+        one.wait()
 
 
 def slots_kernel(dest_ref, weight_ref, slots_ref):
@@ -116,19 +163,6 @@
     slots_ref[0] = total[:rows]
     slots_ref[1] = total[rows : 2 * rows]
     slots_ref[2] = total[2 * rows : 3 * rows] + total[3 * rows :]
-
-
-def table_kernel(disp_ref, vel_ref, table_ref):
-    nodes, width = disp_ref.shape[1], disp_ref.shape[2]
-    half = width // 2
-    for c in range(6):
-        field = disp_ref[c] if c < 3 else vel_ref[c - 3]
-        for n, part in enumerate(split(field.T)):
-            for h in range(2):
-                first = (6 * n + c) * half
-                table_ref[first : first + half, h * nodes : (h + 1) * nodes] = part[
-                    h * half : (h + 1) * half
-                ]
 
 
 def pair(ref, first, start=None):
@@ -277,35 +311,6 @@
             disp_out[c, at, :] = disp_ref[c, at, :] + shell_step * vel_next
 
 
-def pack_kernel(
-    disp_ref, fluid_ref, span_last, span_first, chord_last, chord_first, sems
-):
-    fields, cells_x, cells_y, _ = fluid_ref.shape
-    nodes, width = disp_ref.shape[1], disp_ref.shape[2]
-    copies = []
-
-    def copy(source, target):
-        one = pltpu.make_async_copy(source, target, sems.at[len(copies)])
-        one.start()
-        copies.append(one)
-
-    for c in range(fields):
-        copy(fluid_ref.at[c, pl.ds(cells_x - 3, 3)], span_last.at[pl.ds(3 * c, 3)])
-        copy(fluid_ref.at[c, pl.ds(0, 3)], span_first.at[pl.ds(3 * c, 3)])
-    for n, c in enumerate((0, 2)):
-        copy(fluid_ref.at[c, :, pl.ds(cells_y - 8, 8)], chord_last.at[pl.ds(n * cells_x, cells_x)])
-        copy(fluid_ref.at[c, :, pl.ds(0, 8)], chord_first.at[pl.ds(n * cells_x, cells_x)])
-    for c in range(3):
-        field = disp_ref[c]
-        turned = field.T
-        span_last[3 * fields, c : c + 1, :] = field[nodes - 1 :, :]
-        span_first[3 * fields, c : c + 1, :] = field[:1, :]
-        chord_last[2 * cells_x, c : c + 1, :] = turned[width - 1 :, :]
-        chord_first[2 * cells_x, c : c + 1, :] = turned[:1, :]
-    for one in copies:
-        one.wait()
-
-
 def coef(distance):
     size = jnp.abs(distance)
     value = jnp.where(size == 1, 45.0, jnp.where(size == 2, -9.0, jnp.where(size == 3, 1.0, 0.0)))
@@ -313,7 +318,7 @@
 
 
 def flow_kernel(
-    disp_ref, vel_ref, fluid_ref, before_x, after_x, before_y, after_y,
+    disp_ref, vel_ref, fluid_ref, got_xa, got_xb, got_ya, got_yb,
     next_ref, pressure_ref, surface_ref, shell_ref, wide, tall, normal, held, sems,
 ):
     fields, cells_x, cells_y, length = fluid_ref.shape
@@ -329,12 +334,19 @@
         copy(fluid_ref.at[c], wide.at[c, pl.ds(3, cells_x)])
     for n, c in enumerate((0, 2)):
         copy(fluid_ref.at[c], tall.at[n, :, pl.ds(8, cells_y)])
-    for c in range(fields):
-        wide[c, 0:3] = before_x[3 * c : 3 * c + 3]
-        wide[c, 3 + cells_x : 6 + cells_x] = after_x[3 * c : 3 * c + 3]
-    for n in range(2):
-        tall[n, :, 0:8, :] = before_y[n * cells_x : (n + 1) * cells_x]
-        tall[n, :, 8 + cells_y : 16 + cells_y, :] = after_y[n * cells_x : (n + 1) * cells_x]
+    odd_x = lax.axis_index("span") % 2
+    odd_y = lax.axis_index("chord") % 2
+    for got, side in ((got_xa, 1 - odd_x), (got_xb, odd_x)):
+        for c in range(fields):
+            wide[c, pl.ds(side * (cells_x + 3), 3)] = got[3 * c : 3 * c + 3]
+    for got, side in ((got_ya, 1 - odd_y), (got_yb, odd_y)):
+        first = pl.multiple_of(side * (cells_y + 8), 8)
+        for n in range(2):
+            tall[n, :, pl.ds(first, 8), :] = got[n * cells_x : (n + 1) * cells_x]
+    ends_x = (got_xa[3 * fields, :8, :], got_xb[3 * fields, :8, :])
+    before_x, after_x = jnp.where(odd_x == 1, *ends_x), jnp.where(odd_x == 0, *ends_x)
+    ends_y = (got_ya[2 * cells_x], got_yb[2 * cells_x])
+    before_y, after_y = jnp.where(odd_y == 1, *ends_y), jnp.where(odd_y == 0, *ends_y)
     row = iota((nodes, width), 0)
     lane = iota((nodes, width), 1)
     for c in range(3):
@@ -346,11 +358,11 @@
             high, low = split(only)
             return dot(high, place, TN) + dot(low, place, TN)
 
-        left = column(before_y[2 * cells_x], 0)
-        right = column(after_y[2 * cells_x], width - 1)
-        above = jnp.where(row == 0, before_x[3 * fields, c : c + 1, :], pltpu.roll(field, 1, 0))
+        left = column(before_y, 0)
+        right = column(after_y, width - 1)
+        above = jnp.where(row == 0, before_x[c : c + 1, :], pltpu.roll(field, 1, 0))
         below = jnp.where(
-            row == nodes - 1, after_x[3 * fields, c : c + 1, :], pltpu.roll(field, nodes - 1, 0)
+            row == nodes - 1, after_x[c : c + 1, :], pltpu.roll(field, nodes - 1, 0)
         )
         west = jnp.where(lane == 0, left, pltpu.roll(field, 1, 1))
         east = jnp.where(lane == width - 1, right, pltpu.roll(field, width - 1, 1))
@@ -462,12 +474,44 @@
     hbm = pl.BlockSpec(memory_space=pl.ANY)
 
     near_out = pltpu.VMEM
-    requests, dest = call(
+    span_shape = near_out((3 * fields + 1, cells_y, length), f32)
+    chord_shape = near_out((2 * cells_x + 1, 8, length), f32)
+    requests, dest, table, span_a, span_b, chord_a, chord_b = call(
         functools.partial(route_kernel, devices, capacity),
-        [near_out((rows, LANES), i32), near_out((stencil, points), i32)],
+        [
+            sds((rows, LANES), i32),
+            near_out((stencil, points), i32),
+            near_out((6 * width, 2 * nodes), bf16),
+            span_shape,
+            span_shape,
+            chord_shape,
+            chord_shape,
+        ],
         owners.T,
         node_local.T,
-    )
+        shell_disp,
+        shell_vel,
+        fluid_state,
+        flops=100_000_000,
+        in_specs=[vmem, vmem, hbm, hbm, hbm],
+        out_specs=[hbm] + [vmem] * 6,
+        scratch_shapes=[
+            pltpu.VMEM((rows, LANES), i32),
+            pltpu.VMEM(shell_disp.shape, f32),
+            pltpu.VMEM(shell_vel.shape, f32),
+            pltpu.SemaphoreType.DMA((2 * fields + 7,)),
+        ],
+    )
+
+    def swapped(one, two, axis, size):
+        even = [pair for i in range(0, size - 1, 2) for pair in ((i, i + 1), (i + 1, i))]
+        odd = [pair for i in range(1, size - 1, 2) for pair in ((i, i + 1), (i + 1, i))]
+        first = lax.ppermute(one, axis, even)
+        return first, lax.ppermute(two, axis, odd)
+
+    got_xa, got_xb = swapped(span_a, span_b, "span", span_count)
+    got_ya, got_yb = swapped(chord_a, chord_b, "chord", chord_count)
+
     asked = exchange(requests, devices, 1, chunk_rows, rows, capacity)
 
     slots = call(
@@ -478,27 +522,6 @@
         held=(0,),
         flops=200_000_000,
     )
-    table = call(table_kernel, near_out((6 * width, 2 * nodes), bf16), shell_disp, shell_vel)
-
-    span_shape = near_out((3 * fields + 1, cells_y, length), f32)
-    chord_shape = near_out((2 * cells_x + 1, 8, length), f32)
-    span_last, span_first, chord_last, chord_first = call(
-        pack_kernel,
-        [span_shape, span_shape, chord_shape, chord_shape],
-        shell_disp,
-        fluid_state,
-        in_specs=[vmem, hbm],
-        scratch_shapes=[pltpu.SemaphoreType.DMA((2 * fields + 4,))],
-    )
-
-    def shifted(last, leading, axis, size):
-        up = [(i, i + 1) for i in range(size - 1)]
-        down = [(i + 1, i) for i in range(size - 1)]
-        return lax.ppermute(last, axis, up), lax.ppermute(leading, axis, down)
-
-    before_x, after_x = shifted(span_last, span_first, "span", span_count)
-    before_y, after_y = shifted(chord_last, chord_first, "chord", chord_count)
-
     flow_next, pressure, surface, shell_base = call(
         flow_kernel,
         [
@@ -510,10 +533,10 @@
         shell_disp,
         shell_vel,
         fluid_state,
-        before_x,
-        after_x,
-        before_y,
-        after_y,
+        got_xa,
+        got_xb,
+        got_ya,
+        got_yb,
         flops=300_000_000,
         held=(0, 1, 3, 4, 5, 6),
         in_specs=[vmem, vmem, hbm, vmem, vmem, vmem, vmem],
@@ -528,7 +551,7 @@
     )
 
     picked = call(
-        functools.partial(fetch_kernel, chunk_rows, 4),
+        functools.partial(fetch_kernel, chunk_rows, 32),
         near_out((6 * rows, LANES), f32),
         asked,
         table,
@@ -539,7 +562,7 @@
 
     wall_first = 2.0 * (-45.0 + 9.0 - 1.0) / 60.0
     interface_motion, wall, loads = call(
-        functools.partial(meet_kernel, chunk_rows, 8, -time_step * wall_first),
+        functools.partial(meet_kernel, chunk_rows, 32, -time_step * wall_first),
         [
             sds((6, points), f32),
             near_out((blocks, LANES), f32),
@@ -551,7 +574,7 @@
         normals,
         held=(0, 1, 2, 3),
         flops=300_000_000,
-        scratch_shapes=[pltpu.VMEM((rows // 8, LANES, 8 * LANES), bf16)],
+        scratch_shapes=[pltpu.VMEM((rows // 32, LANES, 32 * LANES), bf16)],
     )
     arrived = exchange(loads, devices, 3, chunk_rows, rows, capacity)
 
@@ -571,7 +594,7 @@
     )
 
     disp_next, vel_next = call(
-        functools.partial(force_kernel, chunk_rows, 8),
+        functools.partial(force_kernel, chunk_rows, 64),
         [sds(shell_disp.shape, f32), sds(shell_vel.shape, f32)],
         arrived,
         asked,

time: 73.4 us -> 61.5 us (0.84)
  blocking collectives: 0 us -> 14.2 us
  starting transfers between devices: 27.1 us -> 13.5 us
  Pallas kernels: 26.8 us -> 19 us
  waiting for transfers between devices: 17.7 us -> 13 us
    all_to_all x0 -> x1, blocking collectives: none -> 14.2 us  [exchange(): lax.all_to_all(value.reshape(shape), AXES, split_axis=0, concat_axis=0, t...]
    all_to_all x3 -> x2, starting transfers between devices: 17.2 us -> 7.87 us  [exchange(): lax.all_to_all(value.reshape(shape), AXES, split_axis=0, concat_axis=0, t...]
    pallas_call x9 -> x7, Pallas kernels: 26.8 us -> 19 us  [call(): pl.pallas_call(kernel, out_shape=outs, cost_estimate=pl.CostEstimate(flop...]
    all_to_all x3 -> x2, waiting for transfers between devices: 12.4 us -> 6.5 us  [exchange(): lax.all_to_all(value.reshape(shape), AXES, split_axis=0, concat_axis=0, t...]
    ppermute x4, starting transfers between devices: 9.89 us -> 5.67 us  [the longest x2 3.94 us: swapped(): return (first, lax.ppermute(two, axis, odd))]
    ppermute x4, waiting for transfers between devices: 5.27 us -> 6.5 us  [the longest x2 6.5 us: swapped(): first = lax.ppermute(one, axis, even)]
  transfers between devices with their start and end apart: 7 -> 6, of which waited for: 4 -> 2; matrix products, arithmetic and copies ran while one was open for 0% -> 0% of each run, Pallas kernels for 15% -> 12%
where the time goes in v1:
time: 61.5 us; the launch traced here: 60.5 us
  Pallas kernels  19 us (31%)
  blocking collectives  14.2 us (23%)
  starting transfers between devices  13.5 us (22%)
  waiting for transfers between devices  13 us (21%)
  between operations  0.74 us (1%)
    pallas_call x7, Pallas kernels, call(): pl.pallas_call(kernel, out_shape=outs, cost_estimate=pl.CostEstimate(flop...  19 us
    all_to_all x1, blocking collectives, exchange(): lax.all_to_all(value.reshape(shape), AXES, split_axis=0, concat_axis=0, t...  14.2 us
    all_to_all x2, starting transfers between devices, exchange(): lax.all_to_all(value.reshape(shape), AXES, split_axis=0, concat_axis=0, t...  7.87 us
    all_to_all x2, waiting for transfers between devices, exchange(): lax.all_to_all(value.reshape(shape), AXES, split_axis=0, concat_axis=0, t...  6.5 us
    ppermute x2, waiting for transfers between devices, swapped(): first = lax.ppermute(one, axis, even)  6.5 us
    ppermute x2, starting transfers between devices, swapped(): return (first, lax.ppermute(two, axis, odd))  3.94 us
    ppermute x2, starting transfers between devices, swapped(): first = lax.ppermute(one, axis, even)  1.73 us
  transfers between devices with their start and end apart: 6, of which 2 were waited for; matrix products, arithmetic and copies ran while one was open for 0% of the time, Pallas kernels for 12%

profile of v1, /device:TPU:1, one launch (start us, length us, event | category | flops | bytes accessed | tf_op | source)
XLA Modules:
  0.0 60.5 jit_solution(3813406721910201688)
XLA Ops:
  0.6 2.6 %shard_map.102 = (s32[64,128]{1,0:T(8,128)}, s32[4,1024]{1,0:T(4,128)S(1)}, bf16[768,256]{1,0:T(8,128)(2,1)S(1)}, f32[13,32,128]{2,1,0:T(8,128)S(1)}, f32[13,32,...) custom-call(s32[4,1024]{1,0:T(4,128)} %bitcast.14, s32[4,1024]{1,0:T(4,128)} %bitcast.15, ...), custom_call_target="tpu_custom_call" | custom-call | flops 100000000 | bytes 2523136 | tf_op jit(solution)/shard_map/pallas_call | solution.py:52
  3.3 14.2 %all_to_all.15 = s32[32,1,256]{2,1,0:T(1,128)S(1)} all-to-all(s32[32,1,256]{2,1,0:T(1,128)} %bitcast.13), channel_id=1, replica_groups=mesh['span'=8,'chord'=4] {'span','chord'}, dimensions={0} | all-to-all | bytes 65536 | tf_op jit(solution)/shard_map/all_to_all | solution.py:454
  17.5 0.0 copy-start
  17.5 0.0 copy-start.1
  17.5 4.2 %shard_map.103 = f32[384,128]{1,0:T(8,128)} custom-call(s32[64,128]{1,0:T(8,128)S(1)} %bitcast.11, bf16[768,256]{1,0:T(8,128)(2,1)S(1)} %get-tuple-element.21.table_ref), custom_call_target="tpu_custom_call" | custom-call | flops 3000000000 | bytes 425984 | tf_op jit(solution)/shard_map/pallas_call | solution.py:52
  21.7 2.6 %all-to-all-start.1 = ((f32[32,1,1536]{2,1,0:T(1,128)}), f32[32,1,1536]{2,1,0:T(1,128)S(1)}, u32[]{:S(2)}, u32[]{:S(2)}) async-start(f32[32,1,1536]{2,1,0:T(1,128)} %bitcast.4), calls=%async_computation.1 | async-start | bytes 393216 | tf_op jit(solution)/shard_map/all_to_all | solution.py:454
  24.3 0.5 collective-permute-start.2
  24.8 3.3 %collective-permute-start.3 = (f32[65,8,128]{2,1,0:T(8,128)S(1)}, f32[65,8,128]{2,1,0:T(8,128)S(1)}, u32[]{:S(2)}, u32[]{:S(2)}) collective-permute-start(f32[65,8,128]{2,1,0:T(8,128)S(1)} %get-tuple-element.26), channel_id=1, source_target_pairs={{1,2},{2,1},{5,6},{6,5},{9,10},{10,9},{13,14},{14,13},{17,18},{18,... | collective-permute-start | bytes 798728 | tf_op jit(solution)/shard_map/ppermute | solution.py:510
  28.0 1.3 %collective-permute-start = (f32[13,32,128]{2,1,0:T(8,128)S(1)}, f32[13,32,128]{2,1,0:T(8,128)S(1)}, u32[]{:S(2)}, u32[]{:S(2)}) collective-permute-start(f32[13,32,128]{2,1,0:T(8,128)S(1)} %get-tuple-element.23), channel_id=1, source_target_pairs={{0,4},{4,0},{8,12},{12,8},{16,20},{20,16},{24,28},{28,24},{1,5},{5... | collective-permute-start | bytes 638984 | tf_op jit(solution)/shard_map/ppermute | solution.py:509
  29.3 0.7 %collective-permute-start.1 = (f32[13,32,128]{2,1,0:T(8,128)S(1)}, f32[13,32,128]{2,1,0:T(8,128)S(1)}, u32[]{:S(2)}, u32[]{:S(2)}) collective-permute-start(f32[13,32,128]{2,1,0:T(8,128)S(1)} %get-tuple-element.24), channel_id=1, source_target_pairs={{4,8},{8,4},{12,16},{16,12},{20,24},{24,20},{5,9},{9,5},{13,17},{1... | collective-permute-start | bytes 638984 | tf_op jit(solution)/shard_map/ppermute | solution.py:510
  30.0 0.0 copy-start.2
  30.0 1.4 %shard_map.104.slots_ref = f32[3,64,128]{2,1,0:T(8,128)S(1)} custom-call(s32[4,1024]{1,0:T(4,128)S(1)} %get-tuple-element.22.dest_ref, f32[4,1024]{1,0:T(4,128)} %bitcast.16), custom_call_target="tpu_custom_call" | custom-call | flops 200000000 | bytes 32768 | tf_op jit(solution)/shard_map/pallas_call | solution.py:52
  31.4 6.5 %collective-permute-done.got_xa = f32[13,32,128]{2,1,0:T(8,128)S(1)} collective-permute-done((f32[13,32,128]{2,1,0:T(8,128)S(1)}, f32[13,32,128]{2,1,0:T(8,128)S(1)}, u32[]{:S(2)}, u32[]{:S(2)}) %collective-permute-start) | collective-permute-done | bytes 213024 | tf_op jit(solution)/shard_map/ppermute | solution.py:509
  37.9 0.0 collective-permute-done.1.got_xb
  37.9 0.0 collective-permute-done.2.got_ya
  37.9 0.0 collective-permute-done.3.got_yb
  37.9 0.0 copy-done
  38.0 0.0 copy-done.1
  38.0 4.6 %shard_map.105 = (f32[4,32,32,128]{3,2,1,0:T(8,128)}, f32[32,32,128]{2,1,0:T(8,128)S(1)}, f32[8,128]{1,0:T(8,128)S(1)}, f32[3,128,128]{2,1,0:T(8,128)S(1)}) custom-call(f32[3,128,128]{2,1,0:T(8,128)S(1)} %copy-done.1, f32[3,128,128]{2,1,0:T(8,128)S(1)} %copy-done, f32[4,32,32,128]{3,2,1,0:T(8,128)} %fluid_ref.3, ...), custom_call_target="tpu_custom_call" | custom-call | flops 300000000 | bytes 3448832 | tf_op jit(solution)/shard_map/pallas_call | solution.py:52
  42.5 0.0 all-to-all-done.1
  42.6 0.0 copy-done.2
  42.6 2.4 %shard_map.106 = (f32[6,1024]{1,0:T(8,128)}, f32[8,128]{1,0:T(8,128)S(1)}, f32[192,128]{1,0:T(8,128)}) custom-call(f32[384,128]{1,0:T(8,128)S(1)} %bitcast.9, f32[3,64,128]{2,1,0:T(8,128)S(1)} %shard_map.104.slots_ref, f32[8,128]{1,0:T(8,128)S(1)} %get-tuple-element.27.base_ref, f32[3,1024]{1,0:T(4,128)S(1)} %copy-done.2), custom_call_target="tpu_custom_call" | custom-call | flops 300000000 | bytes 311296 | tf_op jit(solution)/shard_map/pallas_call | solution.py:52
  45.0 5.3 %all-to-all-start.2 = ((f32[32,1,768]{2,1,0:T(1,128)}), f32[32,1,768]{2,1,0:T(1,128)S(1)}, u32[]{:S(2)}, u32[]{:S(2)}) async-start(f32[32,1,768]{2,1,0:T(1,128)} %bitcast.7), calls=%async_computation.2 | async-start | bytes 196608 | tf_op jit(solution)/shard_map/all_to_all | solution.py:454
  50.3 1.1 %shard_map.107 = f32[4,32,32,128]{3,2,1,0:T(8,128)} custom-call(f32[8,128]{1,0:T(8,128)S(1)} %get-tuple-element.28.wall_ref, f32[32,32,128]{2,1,0:T(8,128)S(1)} %get-tuple-element.29.pressure_ref, f32[4,32,32,128]{3,2,1,0:T(8,128)} %get-tuple-element.30.next_in), custom_call_target="tpu_custom_call", output_to_operand_aliasing={{}: (2, {})} | custom-call | flops 100000000 | bytes 2625536 | tf_op jit(solution)/shard_map/pallas_call | solution.py:52
  51.4 6.5 %all-to-all-done.2 = f32[32,1,768]{2,1,0:T(1,128)S(1)} async-done(((f32[32,1,768]{2,1,0:T(1,128)}), f32[32,1,768]{2,1,0:T(1,128)S(1)}, u32[]{:S(2)}, u32[]{:S(2)}) %all-to-all-start.2) | async-done | bytes 98336 | tf_op jit(solution)/shard_map/all_to_all | solution.py:454
  57.9 2.6 %shard_map.108 = (f32[3,128,128]{2,1,0:T(8,128)}, f32[3,128,128]{2,1,0:T(8,128)}) custom-call(f32[192,128]{1,0:T(8,128)S(1)} %bitcast.10, s32[64,128]{1,0:T(8,128)S(1)} %bitcast.12, f32[3,128,128]{2,1,0:T(8,128)S(1)} %get-tuple-element.33.base_ref, f32[3,128,128]{2,1,0:T(8,128)S(1)} %copy-done.1), custom_call_target="tpu_custom_call" | custom-call | flops 3000000000 | bytes 524288 | tf_op jit(solution)/shard_map/pallas_call | solution.py:52
Async XLA Ops:
  17.5 20.5 %copy-start = (f32[3,128,128]{2,1,0:T(8,128)S(1)}, f32[3,128,128]{2,1,0:T(8,128)}, u32[]{:S(2)}) copy-start(f32[3,128,128]{2,1,0:T(8,128)} %vel_ref.1) | copy-start | bytes 589828
  17.5 20.5 %copy-start.1 = (f32[3,128,128]{2,1,0:T(8,128)S(1)}, f32[3,128,128]{2,1,0:T(8,128)}, u32[]{:S(2)}) copy-start(f32[3,128,128]{2,1,0:T(8,128)} %disp_ref.3) | copy-start | bytes 589828
  21.7 20.8 %all-to-all-start.1 = ((f32[32,1,1536]{2,1,0:T(1,128)}), f32[32,1,1536]{2,1,0:T(1,128)S(1)}, u32[]{:S(2)}, u32[]{:S(2)}) async-start(f32[32,1,1536]{2,1,0:T(1,128)} %bitcast.4), calls=%async_computation.1 | async-start | bytes 393216 | tf_op jit(solution)/shard_map/all_to_all | solution.py:454
  24.3 13.6 %collective-permute-start.2 = (f32[65,8,128]{2,1,0:T(8,128)S(1)}, f32[65,8,128]{2,1,0:T(8,128)S(1)}, u32[]{:S(2)}, u32[]{:S(2)}) collective-permute-start(f32[65,8,128]{2,1,0:T(8,128)S(1)} %get-tuple-element.25), channel_id=1, source_target_pairs={{0,1},{1,0},{2,3},{3,2},{4,5},{5,4},{6,7},{7,6},{8,9},{9,8},{10,11... | collective-permute-start | bytes 798728 | tf_op jit(solution)/shard_map/ppermute | solution.py:509
  24.8 13.2 %collective-permute-start.3 = (f32[65,8,128]{2,1,0:T(8,128)S(1)}, f32[65,8,128]{2,1,0:T(8,128)S(1)}, u32[]{:S(2)}, u32[]{:S(2)}) collective-permute-start(f32[65,8,128]{2,1,0:T(8,128)S(1)} %get-tuple-element.26), channel_id=1, source_target_pairs={{1,2},{2,1},{5,6},{6,5},{9,10},{10,9},{13,14},{14,13},{17,18},{18,... | collective-permute-start | bytes 798728 | tf_op jit(solution)/shard_map/ppermute | solution.py:510
  28.0 9.9 %collective-permute-start = (f32[13,32,128]{2,1,0:T(8,128)S(1)}, f32[13,32,128]{2,1,0:T(8,128)S(1)}, u32[]{:S(2)}, u32[]{:S(2)}) collective-permute-start(f32[13,32,128]{2,1,0:T(8,128)S(1)} %get-tuple-element.23), channel_id=1, source_target_pairs={{0,4},{4,0},{8,12},{12,8},{16,20},{20,16},{24,28},{28,24},{1,5},{5... | collective-permute-start | bytes 638984 | tf_op jit(solution)/shard_map/ppermute | solution.py:509
  29.3 8.6 %collective-permute-start.1 = (f32[13,32,128]{2,1,0:T(8,128)S(1)}, f32[13,32,128]{2,1,0:T(8,128)S(1)}, u32[]{:S(2)}, u32[]{:S(2)}) collective-permute-start(f32[13,32,128]{2,1,0:T(8,128)S(1)} %get-tuple-element.24), channel_id=1, source_target_pairs={{4,8},{8,4},{12,16},{16,12},{20,24},{24,20},{5,9},{9,5},{13,17},{1... | collective-permute-start | bytes 638984 | tf_op jit(solution)/shard_map/ppermute | solution.py:510
  30.0 12.6 %copy-start.2 = (f32[3,1024]{1,0:T(4,128)S(1)}, f32[3,1024]{1,0:T(4,128)}, u32[]{:S(2)}) copy-start(f32[3,1024]{1,0:T(4,128)} %normals_ref.1) | copy-start | bytes 36868
  45.0 13.0 %all-to-all-start.2 = ((f32[32,1,768]{2,1,0:T(1,128)}), f32[32,1,768]{2,1,0:T(1,128)S(1)}, u32[]{:S(2)}, u32[]{:S(2)}) async-start(f32[32,1,768]{2,1,0:T(1,128)} %bitcast.7), calls=%async_computation.2 | async-start | bytes 196608 | tf_op jit(solution)/shard_map/all_to_all | solution.py:454

commit v2 on v1

--- a/solution.py
+++ b/solution.py
@@ -209,39 +209,41 @@
     lax.fori_loop(0, rows // (2 * group), step, 0)
 
 
+def gather_points(chunk_rows, channels, group, got_ref, slots_ref, g, total):
+    rows = slots_ref.shape[1]
+    blocks = total.shape[0] // (2 * len(channels))
+    lefts, hots = [], []
+    for s in range(group):
+        row = g * group + s
+        weight = slots_ref[2, pl.ds(row, 1), :]
+        mine = iota((blocks, LANES), 0).astype(f32) == slots_ref[0, pl.ds(row, 1), :]
+        hots.append(
+            jnp.where(
+                iota((LANES, LANES), 0).astype(f32) == slots_ref[1, pl.ds(row, 1), :], 1.0, 0.0
+            ).astype(bf16)
+        )
+        left = []
+        for c in channels:
+            value = got_ref[pl.ds(position(chunk_rows, 6, rows, c, row), 1), :]
+            for part in split(value * weight):
+                left.append(jnp.where(mine, part.astype(f32), 0.0))
+        lefts.append(jnp.concatenate(left, axis=0).astype(bf16))
+    hots = jnp.concatenate(hots, axis=1)
+    return total + dot(jnp.concatenate(lefts, axis=1), hots, NT), hots
+
+
 def meet_kernel(
-    chunk_rows, group, factor, got_ref, slots_ref, base_ref, normals_ref, motion_ref, wall_ref, out_ref,
-    hot_ref,
+    chunk_rows, group, factor, got_ref, slots_ref, base_ref, normals_ref, wall_ref, out_ref, hot_ref
 ):
     rows = slots_ref.shape[1]
     blocks = base_ref.shape[0]
 
     def gather(g, total):
-        lefts, hots = [], []
-        for s in range(group):
-            row = g * group + s
-            weight = slots_ref[2, pl.ds(row, 1), :]
-            mine = iota((blocks, LANES), 0).astype(f32) == slots_ref[0, pl.ds(row, 1), :]
-            hot = jnp.where(
-                iota((LANES, LANES), 0).astype(f32) == slots_ref[1, pl.ds(row, 1), :], 1.0, 0.0
-            ).astype(bf16)
-            left = []
-            for c in range(6):
-                value = got_ref[pl.ds(position(chunk_rows, 6, rows, c, row), 1), :]
-                for part in split(value * weight):
-                    left.append(jnp.where(mine, part.astype(f32), 0.0))
-            lefts.append(jnp.concatenate(left, axis=0).astype(bf16))
-            hots.append(hot)
-        hot = jnp.concatenate(hots, axis=1)
-        hot_ref[g] = hot
-        return total + dot(jnp.concatenate(lefts, axis=1), hot, NT)
-
-    total = lax.fori_loop(0, rows // group, gather, jnp.zeros((12 * blocks, LANES), f32))
-    for c in range(6):
-        value = total[2 * c * blocks : (2 * c + 1) * blocks] + total[(2 * c + 1) * blocks : (2 * c + 2) * blocks]
-        for a in range(blocks):
-            motion_ref[c : c + 1, a * LANES : (a + 1) * LANES] = value[a : a + 1]
-    wall = value
+        total, hot_ref[g] = gather_points(chunk_rows, (5,), group, got_ref, slots_ref, g, total)
+        return total
+
+    total = lax.fori_loop(0, rows // group, gather, jnp.zeros((2 * blocks, LANES), f32))
+    wall = total[:blocks] + total[blocks:]
     wall_ref[...] = wall
     pressure = base_ref[...] + factor * wall
     left = []
@@ -319,7 +321,7 @@
 
 def flow_kernel(
     disp_ref, vel_ref, fluid_ref, got_xa, got_xb, got_ya, got_yb,
-    next_ref, pressure_ref, surface_ref, shell_ref, wide, tall, normal, held, sems,
+    next_ref, pressure_ref, surface_ref, shell_ref, wide, across, normal, held, sems,
 ):
     fields, cells_x, cells_y, length = fluid_ref.shape
     nodes, width = disp_ref.shape[1], disp_ref.shape[2]
@@ -332,17 +334,11 @@
 
     for c in range(fields):
         copy(fluid_ref.at[c], wide.at[c, pl.ds(3, cells_x)])
-    for n, c in enumerate((0, 2)):
-        copy(fluid_ref.at[c], tall.at[n, :, pl.ds(8, cells_y)])
     odd_x = lax.axis_index("span") % 2
     odd_y = lax.axis_index("chord") % 2
     for got, side in ((got_xa, 1 - odd_x), (got_xb, odd_x)):
         for c in range(fields):
             wide[c, pl.ds(side * (cells_x + 3), 3)] = got[3 * c : 3 * c + 3]
-    for got, side in ((got_ya, 1 - odd_y), (got_yb, odd_y)):
-        first = pl.multiple_of(side * (cells_y + 8), 8)
-        for n in range(2):
-            tall[n, :, pl.ds(first, 8), :] = got[n * cells_x : (n + 1) * cells_x]
     ends_x = (got_xa[3 * fields, :8, :], got_xb[3 * fields, :8, :])
     before_x, after_x = jnp.where(odd_x == 1, *ends_x), jnp.where(odd_x == 0, *ends_x)
     ends_y = (got_ya[2 * cells_x], got_yb[2 * cells_x])
@@ -382,6 +378,25 @@
         total = dot(jnp.concatenate([high, low], axis=1), jnp.concatenate([table, table], axis=0), NN)
         normal[n] = (total * (1.0 / 60.0)).reshape(cells_x, cells_y, length)
 
+    per = LANES // cells_y
+    target = iota((LANES, LANES), 0)
+    source = iota((LANES, LANES), 1)
+    same = jnp.where(target // cells_y == source // cells_y, coef(source - target), 0.0)
+    target = iota((LANES, 8 * per), 0)
+    source = iota((LANES, 8 * per), 1)
+    near_plane = target // cells_y == source // 8
+    below_y = jnp.where(near_plane, coef(source % 8 - 8 - target % cells_y), 0.0)
+    above_y = jnp.where(near_plane, coef(cells_y + source % 8 - target % cells_y), 0.0)
+    chord_table = jnp.concatenate([same, same, below_y, below_y, above_y, above_y], axis=1).astype(bf16)
+    for n, field in enumerate((0, 2)):
+        for g in range(cells_x // per):
+            inner_rows = wide[field, 3 + g * per : 3 + (g + 1) * per].reshape(LANES, length)
+            at = slice(n * cells_x + g * per, n * cells_x + (g + 1) * per)
+            ends = (got_ya[at].reshape(8 * per, length), got_yb[at].reshape(8 * per, length))
+            parts = split(inner_rows) + split(jnp.where(odd_y == 1, *ends)) + split(jnp.where(odd_y == 0, *ends))
+            total = dot(chord_table, jnp.concatenate(parts, axis=0), NN) * (1.0 / 60.0)
+            across[n, g * per : (g + 1) * per] = total.reshape(per, cells_y, length)
+
     def central(window):
         return (
             0.75 * (window(1) - window(-1)) - 0.15 * (window(2) - window(-2))
@@ -391,16 +406,13 @@
         def along_x(field):
             return central(lambda offset: wide[field, x + 3 + offset])
 
-        def along_y(slot):
-            return central(lambda offset: tall[slot, x, 8 + offset : 8 + offset + cells_y, :])
-
         x_p = along_x(0)
         x_u = along_x(1)
         pressure_ref[x] = wide[0, x + 3] + time_step * (
-            -flow_speed * x_p - (x_u + along_y(1) + normal[1, x])
+            -flow_speed * x_p - (x_u + across[1, x] + normal[1, x])
         )
         held[0, x] = wide[1, x + 3] + time_step * (-flow_speed * x_u - x_p)
-        held[1, x] = wide[2, x + 3] + time_step * (-flow_speed * along_x(2) - along_y(0))
+        held[1, x] = wide[2, x + 3] + time_step * (-flow_speed * along_x(2) - across[0, x])
         held[2, x] = wide[3, x + 3] + time_step * (-flow_speed * along_x(3) - normal[0, x])
 
     parts = 4
@@ -420,7 +432,6 @@
         copies.append(one)
     lead = jnp.where((iota((8, length), 0) == 0) & (iota((8, length), 1) == 0), 1.0, 0.0).astype(bf16)
     blocks = surface_ref.shape[0]
-    per = LANES // cells_y
     for b in range(blocks):
         high, low = split(pressure_ref[b * per : (b + 1) * per].reshape(LANES, length))
         found = dot(lead, high, NT) + dot(lead, low, NT)
@@ -429,7 +440,24 @@
         one.wait()
 
 
-def wall_kernel(wall_ref, pressure_ref, next_in, next_out):
+def wall_kernel(
+    chunk_rows, group, got_ref, slots_ref, wall_ref, pressure_ref, next_in, next_out, motion_ref
+):
+    blocks = wall_ref.shape[0]
+    channels = (0, 1, 2, 3, 4)
+
+    def gather(g, total):
+        return gather_points(chunk_rows, channels, group, got_ref, slots_ref, g, total)[0]
+
+    groups = slots_ref.shape[1] // group
+    total = lax.fori_loop(0, groups, gather, jnp.zeros((10 * blocks, LANES), f32))
+    for c in range(6):
+        if c < 5:
+            value = total[2 * c * blocks : (2 * c + 1) * blocks] + total[(2 * c + 1) * blocks : (2 * c + 2) * blocks]
+        else:
+            value = wall_ref[...]
+        for a in range(blocks):
+            motion_ref[c : c + 1, a * LANES : (a + 1) * LANES] = value[a : a + 1]
     del next_in
     _, cells_x, cells_y, length = next_out.shape
     target = iota((8, length), 1)
@@ -543,7 +571,7 @@
         out_specs=[hbm, vmem, vmem, vmem],
         scratch_shapes=[
             pltpu.VMEM((fields, cells_x + 6, cells_y, length), f32),
-            pltpu.VMEM((2, cells_x, cells_y + 16, length), f32),
+            pltpu.VMEM((2, cells_x, cells_y, length), f32),
             pltpu.VMEM((2, cells_x, cells_y, length), f32),
             pltpu.VMEM((3, cells_x, cells_y, length), f32),
             pltpu.SemaphoreType.DMA((fields + 2,)),
@@ -561,12 +589,12 @@
     replies = exchange(picked, devices, 6, chunk_rows, rows, capacity)
 
     wall_first = 2.0 * (-45.0 + 9.0 - 1.0) / 60.0
-    interface_motion, wall, loads = call(
-        functools.partial(meet_kernel, chunk_rows, 32, -time_step * wall_first),
+    group = 32
+    wall, loads = call(
+        functools.partial(meet_kernel, chunk_rows, group, -time_step * wall_first),
         [
-            sds((6, points), f32),
             near_out((blocks, LANES), f32),
-            near_out((3 * rows, LANES), f32),
+            sds((3 * rows, LANES), f32),
         ],
         replies,
         slots,
@@ -574,23 +602,25 @@
         normals,
         held=(0, 1, 2, 3),
         flops=300_000_000,
-        scratch_shapes=[pltpu.VMEM((rows // 32, LANES, 32 * LANES), bf16)],
+        scratch_shapes=[pltpu.VMEM((rows // group, LANES, group * LANES), bf16)],
     )
     arrived = exchange(loads, devices, 3, chunk_rows, rows, capacity)
 
     block = pl.BlockSpec((1, cells_x, cells_y, length), lambda i: (0, 0, 0, 0))
-    fluid_next = call(
-        wall_kernel,
-        sds(fluid_state.shape, f32),
+    fluid_next, interface_motion = call(
+        functools.partial(wall_kernel, chunk_rows, group),
+        [sds(fluid_state.shape, f32), sds((6, points), f32)],
+        replies,
+        slots,
         wall,
         pressure,
         flow_next,
-        flops=100_000_000,
-        held=(0, 1),
+        flops=200_000_000,
+        held=(0, 1, 2, 3),
         grid=(1,),
-        in_specs=[vmem, vmem, hbm],
-        out_specs=block,
-        input_output_aliases={2: 0},
+        in_specs=[vmem, vmem, vmem, vmem, hbm],
+        out_specs=[block, vmem],
+        input_output_aliases={4: 0},
     )
 
     disp_next, vel_next = call(

time: 61.5 us -> 61 us (level)
  waiting for transfers between devices: 13 us -> 12 us
    all_to_all x2, waiting for transfers between devices: 6.5 us -> 5.51 us  [exchange(): lax.all_to_all(value.reshape(shape), AXES, split_axis=0, concat_axis=0, t...]
  transfers between devices with their start and end apart: 6 -> 6, of which waited for: 2 -> 2; matrix products, arithmetic and copies ran while one was open for 0% -> 0% of each run, Pallas kernels for 12% -> 13%
where the time goes in v2:
time: 61 us; the launch traced here: 60 us
  Pallas kernels  19.5 us (32%)
  blocking collectives  14.2 us (23%)
  starting transfers between devices  13.5 us (22%)
  waiting for transfers between devices  12 us (20%)
  between operations  0.74 us (1%)
    pallas_call x7, Pallas kernels, call(): pl.pallas_call(kernel, out_shape=outs, cost_estimate=pl.CostEstimate(flop...  19.5 us
    all_to_all x1, blocking collectives, exchange(): lax.all_to_all(value.reshape(shape), AXES, split_axis=0, concat_axis=0, t...  14.2 us
    all_to_all x2, starting transfers between devices, exchange(): lax.all_to_all(value.reshape(shape), AXES, split_axis=0, concat_axis=0, t...  7.87 us
    ppermute x2, waiting for transfers between devices, swapped(): first = lax.ppermute(one, axis, even)  6.5 us
    all_to_all x2, waiting for transfers between devices, exchange(): lax.all_to_all(value.reshape(shape), AXES, split_axis=0, concat_axis=0, t...  5.51 us
    ppermute x2, starting transfers between devices, swapped(): return (first, lax.ppermute(two, axis, odd))  3.94 us
    ppermute x2, starting transfers between devices, swapped(): first = lax.ppermute(one, axis, even)  1.73 us
  transfers between devices with their start and end apart: 6, of which 2 were waited for; matrix products, arithmetic and copies ran while one was open for 0% of the time, Pallas kernels for 13%

profile of v2, /device:TPU:1, one launch (start us, length us, event | category | flops | bytes accessed | tf_op | source)
XLA Modules:
  0.0 60.0 jit_solution(17224526385728622960)
XLA Ops:
  0.6 2.6 %shard_map.102 = (s32[64,128]{1,0:T(8,128)}, s32[4,1024]{1,0:T(4,128)S(1)}, bf16[768,256]{1,0:T(8,128)(2,1)S(1)}, f32[13,32,128]{2,1,0:T(8,128)S(1)}, f32[13,32,...) custom-call(s32[4,1024]{1,0:T(4,128)} %bitcast.16, s32[4,1024]{1,0:T(4,128)} %bitcast.17, ...), custom_call_target="tpu_custom_call" | custom-call | flops 100000000 | bytes 2523136 | tf_op jit(solution)/shard_map/pallas_call | solution.py:52
  3.3 14.2 %all_to_all.15 = s32[32,1,256]{2,1,0:T(1,128)S(1)} all-to-all(s32[32,1,256]{2,1,0:T(1,128)} %bitcast.15), channel_id=1, replica_groups=mesh['span'=8,'chord'=4] {'span','chord'}, dimensions={0} | all-to-all | bytes 65536 | tf_op jit(solution)/shard_map/all_to_all | solution.py:482
  17.5 0.0 copy-start
  17.5 0.0 copy-start.1
  17.5 4.2 %shard_map.103 = f32[384,128]{1,0:T(8,128)} custom-call(s32[64,128]{1,0:T(8,128)S(1)} %bitcast.12, bf16[768,256]{1,0:T(8,128)(2,1)S(1)} %get-tuple-element.22.table_ref), custom_call_target="tpu_custom_call" | custom-call | flops 3000000000 | bytes 425984 | tf_op jit(solution)/shard_map/pallas_call | solution.py:52
  21.7 2.6 %all-to-all-start.1 = ((f32[32,1,1536]{2,1,0:T(1,128)}), f32[32,1,1536]{2,1,0:T(1,128)S(1)}, u32[]{:S(2)}, u32[]{:S(2)}) async-start(f32[32,1,1536]{2,1,0:T(1,128)} %bitcast.4), calls=%async_computation.1 | async-start | bytes 393216 | tf_op jit(solution)/shard_map/all_to_all | solution.py:482
  24.3 0.5 collective-permute-start.2
  24.8 3.3 %collective-permute-start.3 = (f32[65,8,128]{2,1,0:T(8,128)S(1)}, f32[65,8,128]{2,1,0:T(8,128)S(1)}, u32[]{:S(2)}, u32[]{:S(2)}) collective-permute-start(f32[65,8,128]{2,1,0:T(8,128)S(1)} %get-tuple-element.27), channel_id=1, source_target_pairs={{1,2},{2,1},{5,6},{6,5},{9,10},{10,9},{13,14},{14,13},{17,18},{18,... | collective-permute-start | bytes 798728 | tf_op jit(solution)/shard_map/ppermute | solution.py:538
  28.1 1.3 %collective-permute-start = (f32[13,32,128]{2,1,0:T(8,128)S(1)}, f32[13,32,128]{2,1,0:T(8,128)S(1)}, u32[]{:S(2)}, u32[]{:S(2)}) collective-permute-start(f32[13,32,128]{2,1,0:T(8,128)S(1)} %get-tuple-element.24), channel_id=1, source_target_pairs={{0,4},{4,0},{8,12},{12,8},{16,20},{20,16},{24,28},{28,24},{1,5},{5... | collective-permute-start | bytes 638984 | tf_op jit(solution)/shard_map/ppermute | solution.py:537
  29.3 0.7 %collective-permute-start.1 = (f32[13,32,128]{2,1,0:T(8,128)S(1)}, f32[13,32,128]{2,1,0:T(8,128)S(1)}, u32[]{:S(2)}, u32[]{:S(2)}) collective-permute-start(f32[13,32,128]{2,1,0:T(8,128)S(1)} %get-tuple-element.25), channel_id=1, source_target_pairs={{4,8},{8,4},{12,16},{16,12},{20,24},{24,20},{5,9},{9,5},{13,17},{1... | collective-permute-start | bytes 638984 | tf_op jit(solution)/shard_map/ppermute | solution.py:538
  30.0 0.0 copy-start.2
  30.0 1.4 %shard_map.104.slots_ref = f32[3,64,128]{2,1,0:T(8,128)S(1)} custom-call(s32[4,1024]{1,0:T(4,128)S(1)} %get-tuple-element.23.dest_ref, f32[4,1024]{1,0:T(4,128)} %bitcast.18), custom_call_target="tpu_custom_call" | custom-call | flops 200000000 | bytes 32768 | tf_op jit(solution)/shard_map/pallas_call | solution.py:52
  31.4 6.5 %collective-permute-done.got_xa = f32[13,32,128]{2,1,0:T(8,128)S(1)} collective-permute-done((f32[13,32,128]{2,1,0:T(8,128)S(1)}, f32[13,32,128]{2,1,0:T(8,128)S(1)}, u32[]{:S(2)}, u32[]{:S(2)}) %collective-permute-start) | collective-permute-done | bytes 213024 | tf_op jit(solution)/shard_map/ppermute | solution.py:537
  37.9 0.0 collective-permute-done.1.got_xb
  37.9 0.0 collective-permute-done.2.got_ya
  37.9 0.0 collective-permute-done.3.got_yb
  37.9 0.0 copy-done
  38.0 0.0 copy-done.1
  38.0 4.3 %shard_map.105 = (f32[4,32,32,128]{3,2,1,0:T(8,128)}, f32[32,32,128]{2,1,0:T(8,128)S(1)}, f32[8,128]{1,0:T(8,128)S(1)}, f32[3,128,128]{2,1,0:T(8,128)S(1)}) custom-call(f32[3,128,128]{2,1,0:T(8,128)S(1)} %copy-done.1, f32[3,128,128]{2,1,0:T(8,128)S(1)} %copy-done, f32[4,32,32,128]{3,2,1,0:T(8,128)} %fluid_ref.3, ...), custom_call_target="tpu_custom_call" | custom-call | flops 300000000 | bytes 3448832 | tf_op jit(solution)/shard_map/pallas_call | solution.py:52
  42.3 0.0 all-to-all-done.1
  42.3 0.0 copy-done.2
  42.3 2.2 %shard_map.106 = (f32[8,128]{1,0:T(8,128)S(1)}, f32[192,128]{1,0:T(8,128)}) custom-call(f32[384,128]{1,0:T(8,128)S(1)} %bitcast.9, f32[3,64,128]{2,1,0:T(8,128)S(1)} %shard_map.104.slots_ref, f32[8,128]{1,0:T(8,128)S(1)} %get-tuple-element.28.base_ref, f32[3,1024]{1,0:T(4,128)S(1)} %copy-done.2), custom_call_target="tpu_custom_call" | custom-call | flops 300000000 | bytes 311296 | tf_op jit(solution)/shard_map/pallas_call | solution.py:52
  44.5 5.3 %all-to-all-start.2 = ((f32[32,1,768]{2,1,0:T(1,128)}), f32[32,1,768]{2,1,0:T(1,128)S(1)}, u32[]{:S(2)}, u32[]{:S(2)}) async-start(f32[32,1,768]{2,1,0:T(1,128)} %bitcast.14), calls=%async_computation.2 | async-start | bytes 196608 | tf_op jit(solution)/shard_map/all_to_all | solution.py:482
  49.8 2.1 %shard_map.107 = (f32[4,32,32,128]{3,2,1,0:T(8,128)}, f32[6,1024]{1,0:T(8,128)}) custom-call(f32[384,128]{1,0:T(8,128)S(1)} %bitcast.10, f32[3,64,128]{2,1,0:T(8,128)S(1)} %shard_map.104.slots_ref, f32[8,128]{1,0:T(8,128)S(1)} %get-tuple-element.29.wall_ref, f32[32,32,128]{2,1,0:T(8,128)S(1)} %get-tuple-element.30.pressure_ref, ...), custom_call_target="tpu_custom_call", output_to_operand_aliasing={{0}: (4, {})} | custom-call | flops 200000000 | bytes 2920448 | tf_op jit(solution)/shard_map/pallas_call | solution.py:52
  51.9 5.5 %all-to-all-done.2 = f32[32,1,768]{2,1,0:T(1,128)S(1)} async-done(((f32[32,1,768]{2,1,0:T(1,128)}), f32[32,1,768]{2,1,0:T(1,128)S(1)}, u32[]{:S(2)}, u32[]{:S(2)}) %all-to-all-start.2) | async-done | bytes 98336 | tf_op jit(solution)/shard_map/all_to_all | solution.py:482
  57.4 2.6 %shard_map.108 = (f32[3,128,128]{2,1,0:T(8,128)}, f32[3,128,128]{2,1,0:T(8,128)}) custom-call(f32[192,128]{1,0:T(8,128)S(1)} %bitcast.11, s32[64,128]{1,0:T(8,128)S(1)} %bitcast.13, f32[3,128,128]{2,1,0:T(8,128)S(1)} %get-tuple-element.35.base_ref, f32[3,128,128]{2,1,0:T(8,128)S(1)} %copy-done.1), custom_call_target="tpu_custom_call" | custom-call | flops 3000000000 | bytes 524288 | tf_op jit(solution)/shard_map/pallas_call | solution.py:52
Async XLA Ops:
  17.5 20.5 %copy-start = (f32[3,128,128]{2,1,0:T(8,128)S(1)}, f32[3,128,128]{2,1,0:T(8,128)}, u32[]{:S(2)}) copy-start(f32[3,128,128]{2,1,0:T(8,128)} %vel_ref.1) | copy-start | bytes 589828
  17.5 20.5 %copy-start.1 = (f32[3,128,128]{2,1,0:T(8,128)S(1)}, f32[3,128,128]{2,1,0:T(8,128)}, u32[]{:S(2)}) copy-start(f32[3,128,128]{2,1,0:T(8,128)} %disp_ref.3) | copy-start | bytes 589828
  21.7 20.6 %all-to-all-start.1 = ((f32[32,1,1536]{2,1,0:T(1,128)}), f32[32,1,1536]{2,1,0:T(1,128)S(1)}, u32[]{:S(2)}, u32[]{:S(2)}) async-start(f32[32,1,1536]{2,1,0:T(1,128)} %bitcast.4), calls=%async_computation.1 | async-start | bytes 393216 | tf_op jit(solution)/shard_map/all_to_all | solution.py:482
  24.3 13.6 %collective-permute-start.2 = (f32[65,8,128]{2,1,0:T(8,128)S(1)}, f32[65,8,128]{2,1,0:T(8,128)S(1)}, u32[]{:S(2)}, u32[]{:S(2)}) collective-permute-start(f32[65,8,128]{2,1,0:T(8,128)S(1)} %get-tuple-element.26), channel_id=1, source_target_pairs={{0,1},{1,0},{2,3},{3,2},{4,5},{5,4},{6,7},{7,6},{8,9},{9,8},{10,11... | collective-permute-start | bytes 798728 | tf_op jit(solution)/shard_map/ppermute | solution.py:537
  24.8 13.2 %collective-permute-start.3 = (f32[65,8,128]{2,1,0:T(8,128)S(1)}, f32[65,8,128]{2,1,0:T(8,128)S(1)}, u32[]{:S(2)}, u32[]{:S(2)}) collective-permute-start(f32[65,8,128]{2,1,0:T(8,128)S(1)} %get-tuple-element.27), channel_id=1, source_target_pairs={{1,2},{2,1},{5,6},{6,5},{9,10},{10,9},{13,14},{14,13},{17,18},{18,... | collective-permute-start | bytes 798728 | tf_op jit(solution)/shard_map/ppermute | solution.py:538
  28.1 9.9 %collective-permute-start = (f32[13,32,128]{2,1,0:T(8,128)S(1)}, f32[13,32,128]{2,1,0:T(8,128)S(1)}, u32[]{:S(2)}, u32[]{:S(2)}) collective-permute-start(f32[13,32,128]{2,1,0:T(8,128)S(1)} %get-tuple-element.24), channel_id=1, source_target_pairs={{0,4},{4,0},{8,12},{12,8},{16,20},{20,16},{24,28},{28,24},{1,5},{5... | collective-permute-start | bytes 638984 | tf_op jit(solution)/shard_map/ppermute | solution.py:537
  29.3 8.6 %collective-permute-start.1 = (f32[13,32,128]{2,1,0:T(8,128)S(1)}, f32[13,32,128]{2,1,0:T(8,128)S(1)}, u32[]{:S(2)}, u32[]{:S(2)}) collective-permute-start(f32[13,32,128]{2,1,0:T(8,128)S(1)} %get-tuple-element.25), channel_id=1, source_target_pairs={{4,8},{8,4},{12,16},{16,12},{20,24},{24,20},{5,9},{9,5},{13,17},{1... | collective-permute-start | bytes 638984 | tf_op jit(solution)/shard_map/ppermute | solution.py:538
  30.0 12.3 %copy-start.2 = (f32[3,1024]{1,0:T(4,128)S(1)}, f32[3,1024]{1,0:T(4,128)}, u32[]{:S(2)}) copy-start(f32[3,1024]{1,0:T(4,128)} %normals_ref.1) | copy-start | bytes 36868
  44.5 13.0 %all-to-all-start.2 = ((f32[32,1,768]{2,1,0:T(1,128)}), f32[32,1,768]{2,1,0:T(1,128)S(1)}, u32[]{:S(2)}, u32[]{:S(2)}) async-start(f32[32,1,768]{2,1,0:T(1,128)} %bitcast.14), calls=%async_computation.2 | async-start | bytes 196608 | tf_op jit(solution)/shard_map/all_to_all | solution.py:482

commit v3 on v2

--- a/solution.py
+++ b/solution.py
@@ -125,6 +125,7 @@
     copies[1].wait()
     nodes, width = disp_ref.shape[1], disp_ref.shape[2]
     half = width // 2
+    channels = table_ref.shape[0] // (2 * half)
     for c in range(6):
         field = disp_ref[c] if c < 3 else vel_ref[c - 3]
         turned = field.T
@@ -136,8 +137,8 @@
             chord_a[2 * cells_x, c : c + 1, :] = jnp.where(odd_y == 0, *ends)
             chord_b[2 * cells_x, c : c + 1, :] = jnp.where(odd_y == 1, *ends)
         for n, part in enumerate(split(turned)):
-            for h in range(2):
-                first = (6 * n + c) * half
+            for h in range(2 if c >= 6 - channels else 0):
+                first = (channels * n + c - 6 + channels) * half
                 table_ref[first : first + half, h * nodes : (h + 1) * nodes] = part[
                     h * half : (h + 1) * half
                 ]
@@ -179,11 +180,12 @@
     return channel * rows + row
 
 
-def fetch_kernel(chunk_rows, group, asked_ref, table_ref, out_ref):
+def fetch_kernel(chunk_rows, group, asked_ref, table_ref, disp_ref, out_ref):
     rows = asked_ref.shape[0]
-    half = table_ref.shape[0] // 12
-    double = table_ref.shape[1]
-    nodes = double // 2
+    nodes, width = disp_ref.shape[1], disp_ref.shape[2]
+    half = width // 2
+    channels = table_ref.shape[0] // (2 * half)
+    straight = 6 - channels
 
     def step(g, carry):
         for s in range(group):
@@ -193,17 +195,32 @@
             upper = asked // LANES - 1
             second = lower >= half
             at = jnp.where(upper < 0, -1, jnp.where(second, upper + nodes, upper))
-            hot = jnp.where(iota((double, 2 * LANES), 0) == at, 1.0, 0.0).astype(bf16)
+            hot = jnp.where(iota((2 * nodes, 2 * LANES), 0) == at, 1.0, 0.0).astype(bf16)
             picked = dot(table_ref[...], hot, NN)
-            picked = picked[: 6 * half] + picked[6 * half :]
+            picked = picked[: channels * half] + picked[channels * half :]
             keep = iota((half, 2 * LANES), 0) == jnp.where(second, lower - half, lower)
-            for c in range(6):
+            for c in range(channels):
                 found = jnp.sum(
                     jnp.where(keep, picked[c * half : (c + 1) * half], 0.0), axis=0, keepdims=True
                 )
                 for h in range(2):
+                    to = position(chunk_rows, 6, rows, straight + c, 2 * t + h)
+                    out_ref[pl.ds(to, 1), :] = found[:, h * LANES : (h + 1) * LANES]
+            for h in range(2):
+                one = asked_ref[pl.ds(2 * t + h, 1), :]
+                lane = jnp.broadcast_to(one % LANES, (8, LANES))
+                line = one // LANES - 1
+                for c in range(straight):
+                    total = jnp.zeros((8, LANES), f32)
+                    for block in range(nodes // 8):
+                        seen = jnp.take_along_axis(
+                            disp_ref[c, block * 8 : (block + 1) * 8, :], lane, axis=1,
+                            mode="promise_in_bounds",
+                        )
+                        here = iota((8, LANES), 0) + block * 8 == line
+                        total = jnp.where(here, seen, total)
                     to = position(chunk_rows, 6, rows, c, 2 * t + h)
-                    out_ref[pl.ds(to, 1), :] = found[:, h * LANES : (h + 1) * LANES]
+                    out_ref[pl.ds(to, 1), :] = jnp.sum(total, axis=0, keepdims=True)
         return carry
 
     lax.fori_loop(0, rows // (2 * group), step, 0)
@@ -502,6 +519,7 @@
     hbm = pl.BlockSpec(memory_space=pl.ANY)
 
     near_out = pltpu.VMEM
+    straight = 1
     span_shape = near_out((3 * fields + 1, cells_y, length), f32)
     chord_shape = near_out((2 * cells_x + 1, 8, length), f32)
     requests, dest, table, span_a, span_b, chord_a, chord_b = call(
@@ -509,7 +527,7 @@
         [
             sds((rows, LANES), i32),
             near_out((stencil, points), i32),
-            near_out((6 * width, 2 * nodes), bf16),
+            near_out(((6 - straight) * width, 2 * nodes), bf16),
             span_shape,
             span_shape,
             chord_shape,
@@ -583,7 +601,8 @@
         near_out((6 * rows, LANES), f32),
         asked,
         table,
-        held=(0, 1),
+        shell_disp,
+        held=(0, 1, 2),
         flops=3_000_000_000,
     )
     replies = exchange(picked, devices, 6, chunk_rows, rows, capacity)

time: 61 us -> 60.9 us (level)
  no operation moved by 1% of the time
where the time goes in v3:
time: 60.9 us; the launch traced here: 60 us
  Pallas kernels  19.5 us (32%)
  blocking collectives  14.2 us (23%)
  starting transfers between devices  13.5 us (22%)
  waiting for transfers between devices  12 us (20%)
  between operations  0.74 us (1%)
    pallas_call x7, Pallas kernels, call(): pl.pallas_call(kernel, out_shape=outs, cost_estimate=pl.CostEstimate(flop...  19.5 us
    all_to_all x1, blocking collectives, exchange(): lax.all_to_all(value.reshape(shape), AXES, split_axis=0, concat_axis=0, t...  14.2 us
    all_to_all x2, starting transfers between devices, exchange(): lax.all_to_all(value.reshape(shape), AXES, split_axis=0, concat_axis=0, t...  7.87 us
    ppermute x2, waiting for transfers between devices, swapped(): first = lax.ppermute(one, axis, even)  6.5 us
    all_to_all x2, waiting for transfers between devices, exchange(): lax.all_to_all(value.reshape(shape), AXES, split_axis=0, concat_axis=0, t...  5.51 us
    ppermute x2, starting transfers between devices, swapped(): return (first, lax.ppermute(two, axis, odd))  3.94 us
    ppermute x2, starting transfers between devices, swapped(): first = lax.ppermute(one, axis, even)  1.73 us
  transfers between devices with their start and end apart: 6, of which 2 were waited for; matrix products, arithmetic and copies ran while one was open for 0% of the time, Pallas kernels for 13%

profile of v3, /device:TPU:1, one launch (start us, length us, event | category | flops | bytes accessed | tf_op | source)
XLA Modules:
  0.0 60.0 jit_solution(7418733658132939550)
XLA Ops:
  0.6 0.0 copy-start.1
  0.6 2.7 %shard_map.102 = (s32[64,128]{1,0:T(8,128)}, s32[4,1024]{1,0:T(4,128)S(1)}, bf16[640,256]{1,0:T(8,128)(2,1)S(1)}, f32[13,32,128]{2,1,0:T(8,128)S(1)}, f32[13,32,...) custom-call(s32[4,1024]{1,0:T(4,128)} %bitcast.16, s32[4,1024]{1,0:T(4,128)} %bitcast.17, ...), custom_call_target="tpu_custom_call" | custom-call | flops 100000000 | bytes 2523136 | tf_op jit(solution)/shard_map/pallas_call | solution.py:52
  3.3 14.2 %all_to_all.15 = s32[32,1,256]{2,1,0:T(1,128)S(1)} all-to-all(s32[32,1,256]{2,1,0:T(1,128)} %bitcast.15), channel_id=1, replica_groups=mesh['span'=8,'chord'=4] {'span','chord'}, dimensions={0} | all-to-all | bytes 65536 | tf_op jit(solution)/shard_map/all_to_all | solution.py:499
  17.5 0.0 copy-done.1
  17.5 0.0 copy-start
  17.5 4.2 %shard_map.103 = f32[384,128]{1,0:T(8,128)} custom-call(s32[64,128]{1,0:T(8,128)S(1)} %bitcast.12, bf16[640,256]{1,0:T(8,128)(2,1)S(1)} %get-tuple-element.22.table_ref, f32[3,128,128]{2,1,0:T(8,128)S(1)} %copy-done.1), custom_call_target="tpu_custom_call" | custom-call | flops 3000000000 | bytes 557056 | tf_op jit(solution)/shard_map/pallas_call | solution.py:52
  21.7 2.6 %all-to-all-start.1 = ((f32[32,1,1536]{2,1,0:T(1,128)}), f32[32,1,1536]{2,1,0:T(1,128)S(1)}, u32[]{:S(2)}, u32[]{:S(2)}) async-start(f32[32,1,1536]{2,1,0:T(1,128)} %bitcast.4), calls=%async_computation.1 | async-start | bytes 393216 | tf_op jit(solution)/shard_map/all_to_all | solution.py:499
  24.3 0.5 collective-permute-start.2
  24.8 3.3 %collective-permute-start.3 = (f32[65,8,128]{2,1,0:T(8,128)S(1)}, f32[65,8,128]{2,1,0:T(8,128)S(1)}, u32[]{:S(2)}, u32[]{:S(2)}) collective-permute-start(f32[65,8,128]{2,1,0:T(8,128)S(1)} %get-tuple-element.27), channel_id=1, source_target_pairs={{1,2},{2,1},{5,6},{6,5},{9,10},{10,9},{13,14},{14,13},{17,18},{18,... | collective-permute-start | bytes 798728 | tf_op jit(solution)/shard_map/ppermute | solution.py:556
  28.1 1.3 %collective-permute-start = (f32[13,32,128]{2,1,0:T(8,128)S(1)}, f32[13,32,128]{2,1,0:T(8,128)S(1)}, u32[]{:S(2)}, u32[]{:S(2)}) collective-permute-start(f32[13,32,128]{2,1,0:T(8,128)S(1)} %get-tuple-element.24), channel_id=1, source_target_pairs={{0,4},{4,0},{8,12},{12,8},{16,20},{20,16},{24,28},{28,24},{1,5},{5... | collective-permute-start | bytes 638984 | tf_op jit(solution)/shard_map/ppermute | solution.py:555
  29.3 0.7 %collective-permute-start.1 = (f32[13,32,128]{2,1,0:T(8,128)S(1)}, f32[13,32,128]{2,1,0:T(8,128)S(1)}, u32[]{:S(2)}, u32[]{:S(2)}) collective-permute-start(f32[13,32,128]{2,1,0:T(8,128)S(1)} %get-tuple-element.25), channel_id=1, source_target_pairs={{4,8},{8,4},{12,16},{16,12},{20,24},{24,20},{5,9},{9,5},{13,17},{1... | collective-permute-start | bytes 638984 | tf_op jit(solution)/shard_map/ppermute | solution.py:556
  30.0 0.0 copy-start.2
  30.0 1.4 %shard_map.104.slots_ref = f32[3,64,128]{2,1,0:T(8,128)S(1)} custom-call(s32[4,1024]{1,0:T(4,128)S(1)} %get-tuple-element.23.dest_ref, f32[4,1024]{1,0:T(4,128)} %bitcast.18), custom_call_target="tpu_custom_call" | custom-call | flops 200000000 | bytes 32768 | tf_op jit(solution)/shard_map/pallas_call | solution.py:52
  31.5 6.5 %collective-permute-done.got_xa = f32[13,32,128]{2,1,0:T(8,128)S(1)} collective-permute-done((f32[13,32,128]{2,1,0:T(8,128)S(1)}, f32[13,32,128]{2,1,0:T(8,128)S(1)}, u32[]{:S(2)}, u32[]{:S(2)}) %collective-permute-start) | collective-permute-done | bytes 213024 | tf_op jit(solution)/shard_map/ppermute | solution.py:555
  38.0 0.0 collective-permute-done.1.got_xb
  38.0 0.0 collective-permute-done.2.got_ya
  38.0 0.0 collective-permute-done.3.got_yb
  38.0 0.0 copy-done
  38.0 4.3 %shard_map.105 = (f32[4,32,32,128]{3,2,1,0:T(8,128)}, f32[32,32,128]{2,1,0:T(8,128)S(1)}, f32[8,128]{1,0:T(8,128)S(1)}, f32[3,128,128]{2,1,0:T(8,128)S(1)}) custom-call(f32[3,128,128]{2,1,0:T(8,128)S(1)} %copy-done.1, f32[3,128,128]{2,1,0:T(8,128)S(1)} %copy-done, f32[4,32,32,128]{3,2,1,0:T(8,128)} %fluid_ref.3, ...), custom_call_target="tpu_custom_call" | custom-call | flops 300000000 | bytes 3448832 | tf_op jit(solution)/shard_map/pallas_call | solution.py:52
  42.3 0.0 all-to-all-done.1
  42.3 0.0 copy-done.2
  42.3 2.2 %shard_map.106 = (f32[8,128]{1,0:T(8,128)S(1)}, f32[192,128]{1,0:T(8,128)}) custom-call(f32[384,128]{1,0:T(8,128)S(1)} %bitcast.9, f32[3,64,128]{2,1,0:T(8,128)S(1)} %shard_map.104.slots_ref, f32[8,128]{1,0:T(8,128)S(1)} %get-tuple-element.28.base_ref, f32[3,1024]{1,0:T(4,128)S(1)} %copy-done.2), custom_call_target="tpu_custom_call" | custom-call | flops 300000000 | bytes 311296 | tf_op jit(solution)/shard_map/pallas_call | solution.py:52
  44.5 5.3 %all-to-all-start.2 = ((f32[32,1,768]{2,1,0:T(1,128)}), f32[32,1,768]{2,1,0:T(1,128)S(1)}, u32[]{:S(2)}, u32[]{:S(2)}) async-start(f32[32,1,768]{2,1,0:T(1,128)} %bitcast.14), calls=%async_computation.2 | async-start | bytes 196608 | tf_op jit(solution)/shard_map/all_to_all | solution.py:499
  49.8 2.1 %shard_map.107 = (f32[4,32,32,128]{3,2,1,0:T(8,128)}, f32[6,1024]{1,0:T(8,128)}) custom-call(f32[384,128]{1,0:T(8,128)S(1)} %bitcast.10, f32[3,64,128]{2,1,0:T(8,128)S(1)} %shard_map.104.slots_ref, f32[8,128]{1,0:T(8,128)S(1)} %get-tuple-element.29.wall_ref, f32[32,32,128]{2,1,0:T(8,128)S(1)} %get-tuple-element.30.pressure_ref, ...), custom_call_target="tpu_custom_call", output_to_operand_aliasing={{0}: (4, {})} | custom-call | flops 200000000 | bytes 2920448 | tf_op jit(solution)/shard_map/pallas_call | solution.py:52
  51.9 5.5 %all-to-all-done.2 = f32[32,1,768]{2,1,0:T(1,128)S(1)} async-done(((f32[32,1,768]{2,1,0:T(1,128)}), f32[32,1,768]{2,1,0:T(1,128)S(1)}, u32[]{:S(2)}, u32[]{:S(2)}) %all-to-all-start.2) | async-done | bytes 98336 | tf_op jit(solution)/shard_map/all_to_all | solution.py:499
  57.4 2.6 %shard_map.108 = (f32[3,128,128]{2,1,0:T(8,128)}, f32[3,128,128]{2,1,0:T(8,128)}) custom-call(f32[192,128]{1,0:T(8,128)S(1)} %bitcast.11, s32[64,128]{1,0:T(8,128)S(1)} %bitcast.13, f32[3,128,128]{2,1,0:T(8,128)S(1)} %get-tuple-element.35.base_ref, f32[3,128,128]{2,1,0:T(8,128)S(1)} %copy-done.1), custom_call_target="tpu_custom_call" | custom-call | flops 3000000000 | bytes 524288 | tf_op jit(solution)/shard_map/pallas_call | solution.py:52
Async XLA Ops:
  0.6 16.9 %copy-start.1 = (f32[3,128,128]{2,1,0:T(8,128)S(1)}, f32[3,128,128]{2,1,0:T(8,128)}, u32[]{:S(2)}) copy-start(f32[3,128,128]{2,1,0:T(8,128)} %disp_ref.5) | copy-start | bytes 589828
  17.5 20.4 %copy-start = (f32[3,128,128]{2,1,0:T(8,128)S(1)}, f32[3,128,128]{2,1,0:T(8,128)}, u32[]{:S(2)}) copy-start(f32[3,128,128]{2,1,0:T(8,128)} %vel_ref.1) | copy-start | bytes 589828
  21.7 20.5 %all-to-all-start.1 = ((f32[32,1,1536]{2,1,0:T(1,128)}), f32[32,1,1536]{2,1,0:T(1,128)S(1)}, u32[]{:S(2)}, u32[]{:S(2)}) async-start(f32[32,1,1536]{2,1,0:T(1,128)} %bitcast.4), calls=%async_computation.1 | async-start | bytes 393216 | tf_op jit(solution)/shard_map/all_to_all | solution.py:499
  24.3 13.6 %collective-permute-start.2 = (f32[65,8,128]{2,1,0:T(8,128)S(1)}, f32[65,8,128]{2,1,0:T(8,128)S(1)}, u32[]{:S(2)}, u32[]{:S(2)}) collective-permute-start(f32[65,8,128]{2,1,0:T(8,128)S(1)} %get-tuple-element.26), channel_id=1, source_target_pairs={{0,1},{1,0},{2,3},{3,2},{4,5},{5,4},{6,7},{7,6},{8,9},{9,8},{10,11... | collective-permute-start | bytes 798728 | tf_op jit(solution)/shard_map/ppermute | solution.py:555
  24.8 13.2 %collective-permute-start.3 = (f32[65,8,128]{2,1,0:T(8,128)S(1)}, f32[65,8,128]{2,1,0:T(8,128)S(1)}, u32[]{:S(2)}, u32[]{:S(2)}) collective-permute-start(f32[65,8,128]{2,1,0:T(8,128)S(1)} %get-tuple-element.27), channel_id=1, source_target_pairs={{1,2},{2,1},{5,6},{6,5},{9,10},{10,9},{13,14},{14,13},{17,18},{18,... | collective-permute-start | bytes 798728 | tf_op jit(solution)/shard_map/ppermute | solution.py:556
  28.1 9.9 %collective-permute-start = (f32[13,32,128]{2,1,0:T(8,128)S(1)}, f32[13,32,128]{2,1,0:T(8,128)S(1)}, u32[]{:S(2)}, u32[]{:S(2)}) collective-permute-start(f32[13,32,128]{2,1,0:T(8,128)S(1)} %get-tuple-element.24), channel_id=1, source_target_pairs={{0,4},{4,0},{8,12},{12,8},{16,20},{20,16},{24,28},{28,24},{1,5},{5... | collective-permute-start | bytes 638984 | tf_op jit(solution)/shard_map/ppermute | solution.py:555
  29.3 8.6 %collective-permute-start.1 = (f32[13,32,128]{2,1,0:T(8,128)S(1)}, f32[13,32,128]{2,1,0:T(8,128)S(1)}, u32[]{:S(2)}, u32[]{:S(2)}) collective-permute-start(f32[13,32,128]{2,1,0:T(8,128)S(1)} %get-tuple-element.25), channel_id=1, source_target_pairs={{4,8},{8,4},{12,16},{16,12},{20,24},{24,20},{5,9},{9,5},{13,17},{1... | collective-permute-start | bytes 638984 | tf_op jit(solution)/shard_map/ppermute | solution.py:556
  30.0 12.3 %copy-start.2 = (f32[3,1024]{1,0:T(4,128)S(1)}, f32[3,1024]{1,0:T(4,128)}, u32[]{:S(2)}) copy-start(f32[3,1024]{1,0:T(4,128)} %normals_ref.1) | copy-start | bytes 36868
  44.5 13.0 %all-to-all-start.2 = ((f32[32,1,768]{2,1,0:T(1,128)}), f32[32,1,768]{2,1,0:T(1,128)S(1)}, u32[]{:S(2)}, u32[]{:S(2)}) async-start(f32[32,1,768]{2,1,0:T(1,128)} %bitcast.14), calls=%async_computation.2 | async-start | bytes 196608 | tf_op jit(solution)/shard_map/all_to_all | solution.py:499
